TPU v7x, 32 devices: a whole 2x2x4 slice. The times are simulated.
32 devices in a mesh: gz: 8 (over z, x), gy: 4 (over y, core).
Axes of the slice: x: 2, y: 2, z: 4, core: 2. Of those that a mesh axis runs over, the one named last changes fastest.
Arguments:
- right_side: float32 [64, 32, 256], P('gz', 'gy'), may hold values from -10 to 10, as said below
Outputs:
- solution_field: float32 [64, 32, 256], P('gz', 'gy')
- residual: float32 [64, 32, 256], P('gz', 'gy')
Inputs may be any that keep to these rules, and one draw needn't show every extreme that they name: `right_side`: a right-hand side.
All inputs are finite; a program needn't handle non-finite values.
Results may differ from a plain program's by a relative error of at most 0.00015.
Values sent between devices are 32-bit elements; how exact they have to be, the bound alone decides.
A program may use at most 64 MiB of HBM per device.

v0:
```python
import functools

import jax
import jax.numpy as jnp
from jax import lax
from jax.experimental import pallas as pl
from jax.experimental.pallas import tpu as pltpu
from jax.sharding import PartitionSpec as P

MESH = pl.DeviceIdType.MESH
F32 = jnp.float32

LOW0, LOW1, LOW2 = 4, 6, 2
EVENS, ODDS = 9, 8
WINDOW = EVENS + ODDS

PHASE_A = ((0, (0, 1)), (1, (0, 1)))
PHASE_B = ((0, (0, 1)), (1, (0, 1, 0)), (0, (1, 0)))
PHASE_C = ((1, (1, 0)), (0, (1, 0)))

CHUNK0 = 3
CHUNK1 = 9


def add(*terms):
    total = None
    for term in terms:
        if term is not None:
            total = term if total is None else total + term
    return total


def shift(x, axis, step):
    if x is None:
        return None
    size = x.shape[axis]
    moved = pltpu.roll(x, step % size, axis)
    index = lax.broadcasted_iota(jnp.int32, x.shape, axis)
    keep = index >= step if step > 0 else index < size + step
    return jnp.where(keep, moved, 0.0)


def pair_sum(other, parity, axis):
    return add(other, shift(other, axis, 1 if parity == 0 else -1))


def both_sides(x, axis, step):
    return add(shift(x, axis, step), shift(x, axis, -step))


def scale_rows(shape, first, count):
    row = first + 2 * lax.broadcasted_iota(jnp.int32, shape, 0)
    return jnp.where((row >= 0) & (row < count), F32(1.0 / 26.0), F32(0.0))


def box0(s):
    tall = [[add(s[yp][xp], pair_sum(s[1 - yp][xp], yp, 1)) for xp in (0, 1)] for yp in (0, 1)]
    return [[add(tall[yp][xp], pair_sum(tall[yp][1 - xp], xp, 2)) for xp in (0, 1)] for yp in (0, 1)]


def phase0(v, g, scale, steps):
    v = [list(v[0]), list(v[1])]
    for yp, order in steps:
        w = [pair_sum(v[1 - yp][xp], yp, 1) for xp in (0, 1)]
        for xp in order:
            side = pair_sum(add(w[1 - xp], v[yp][1 - xp]), xp, 2)
            v[yp][xp] = add(g[yp][xp], w[xp], side) * scale
    return v


def box1(s):
    tall = [add(s[yp], pair_sum(s[1 - yp], yp, 1)) for yp in (0, 1)]
    return [add(t, both_sides(t, 2, 1)) for t in tall]


def phase1(v, g, scale, steps):
    v = list(v)
    shape = scale.shape
    parity = lax.broadcasted_iota(jnp.int32, shape, 2) % 2
    for yp, order in steps:
        w = pair_sum(v[1 - yp], yp, 1)
        for xp in order:
            new = add(g[yp], w, both_sides(add(w, v[yp]), 2, 1)) * scale
            v[yp] = jnp.where(parity == xp, new, 0.0 if v[yp] is None else v[yp])
    return v


def box2(s):
    if s is None:
        return None
    tall = add(s, both_sides(s, 1, 1))
    return add(tall, both_sides(tall, 2, 2))


def phase2(v, g, scale, steps):
    shape = scale.shape
    y_par = lax.broadcasted_iota(jnp.int32, shape, 1) % 2
    x_par = (lax.broadcasted_iota(jnp.int32, shape, 2) // 2) % 2
    for yp, order in steps:
        w = both_sides(v, 1, 1)
        for xp in order:
            new = add(g, w, both_sides(add(w, v), 2, 2)) * scale
            v = jnp.where((y_par == yp) & (x_par == xp), new, 0.0 if v is None else v)
    return v


def chunks(low, high, size):
    for start in range(low, high, size):
        yield start, min(size, high - start)


YX = [(0, 0), (0, 1), (1, 0), (1, 1)]


def run0(v, f, z0, z_count, odd, low, high, steps, fresh):
    for at, n in chunks(low, high, CHUNK0):
        here = pl.ds(at, n)
        below, above = (pl.ds(at, n), pl.ds(at + 1, n)) if odd else (pl.ds(at - 1, n), pl.ds(at, n))
        rhs = [[f[odd][yp, xp, here] for xp in (0, 1)] for yp in (0, 1)]
        shape = rhs[0][0].shape
        scale = scale_rows(shape, z0 + 2 * at - LOW0 + odd, z_count)
        g = rhs
        if fresh > 0:
            s = [[v[1 - odd][yp, xp, below] + v[1 - odd][yp, xp, above] for xp in (0, 1)] for yp in (0, 1)]
            b = box0(s)
            g = [[rhs[yp][xp] + b[yp][xp] for xp in (0, 1)] for yp in (0, 1)]
        old = [[v[odd][yp, xp, here] if fresh > 1 else None for xp in (0, 1)] for yp in (0, 1)]
        new = phase0(old, g, scale, steps)
        for yp, xp in YX:
            v[odd][yp, xp, here] = new[yp][xp]


def run1(v, f, z0, z_count, odd, low, high, steps, fresh):
    for at, n in chunks(low, high, CHUNK1):
        here = pl.ds(at, n)
        below, above = (pl.ds(at, n), pl.ds(at + 1, n)) if odd else (pl.ds(at - 1, n), pl.ds(at, n))
        g = [f[odd, yp, here] for yp in (0, 1)]
        scale = scale_rows(g[0].shape, z0 + 2 * at - LOW1 + odd, z_count)
        if fresh > 0:
            b = box1([v[1 - odd][yp, below] + v[1 - odd][yp, above] for yp in (0, 1)])
            g = [g[yp] + b[yp] for yp in (0, 1)]
        old = [v[odd][yp, here] if fresh > 1 else None for yp in (0, 1)]
        new = phase1(old, g, scale, steps)
        for yp in (0, 1):
            v[odd][yp, here] = new[yp]


def permutation(size, inverse):
    half = size // 2
    wide = lax.broadcasted_iota(jnp.int32, (size, size), 0 if inverse else 1)
    tall = lax.broadcasted_iota(jnp.int32, (size, size), 1 if inverse else 0)
    source = jnp.where(wide < half, 2 * wide, 2 * (wide - half) + 1)
    return jnp.where(tall == source, F32(1.0), F32(0.0))


def kernel(
    gz_n, gy_n, rhs_hbm, sol_ref, res_ref,
    flat, mine, got, fe, fo, ve, vo, dbuf, cmine, cgot, f1, v1e, v1o, vc, part, parts, nat,
    s1, r1, s2, r2, s3, r3, s4, rhs_ref, s5,
):
    gz, gy = lax.axis_index("gz"), lax.axis_index("gy")
    zl, yl, nx = rhs_ref.shape
    fetch = pltpu.make_async_copy(rhs_hbm, rhs_ref, s5)
    fetch.start()
    y2, x2 = yl // 2, nx // 2
    yc = y2 // 2
    zc = zl // 2
    z_count = gz_n * zl
    z0 = gz * zl
    f, v = (fe, fo), (ve, vo)
    v1 = (v1e, v1o)

    def there(dz):
        return (gz + dz >= 0) & (gz + dz < gz_n)

    barrier = pltpu.get_barrier_semaphore()
    count = jnp.int32(0)
    for dz in range(1 - gz_n, gz_n):
        for dg in range(gy_n if abs(dz) <= 2 else 1):
            if dz == 0 and dg == 0:
                continue

            @pl.when(there(dz))
            def _(dz=dz, dg=dg):
                pl.semaphore_signal(
                    barrier, inc=1, device_id=(gz + dz, lax.rem(gy + dg, gy_n)), device_id_type=MESH
                )

            count = count + there(dz).astype(jnp.int32)

    fetch.wait()
    split = jnp.dot(
        rhs_ref[...].reshape(zl * yl, nx), permutation(nx, False),
        precision=lax.Precision.HIGHEST, preferred_element_type=F32,
    )
    for xp in (0, 1):
        flat[xp] = split[:, xp * x2 : (xp + 1) * x2]
    for z in range(zl):
        for yp, xp in YX:
            row = flat[xp, pl.ds(z * yl + yp, y2, stride=2), :]
            mine[z, (yp * 2 + xp) * y2 : (yp * 2 + xp + 1) * y2, :] = row
    got[gy, pl.ds(LOW0, zl)] = mine[...]

    @pl.when(gz == 0)
    def _():
        got[:, 0:LOW0] = jnp.zeros((gy_n, LOW0) + got.shape[2:], F32)

    @pl.when(gz == gz_n - 1)
    def _():
        got[:, LOW0 + zl :] = jnp.zeros((gy_n, WINDOW - LOW0 - zl) + got.shape[2:], F32)

    high = WINDOW - LOW0 - zl
    moves1 = {-1: (0, high, LOW0 + zl), 0: (0, zl, LOW0), 1: (zl - LOW0, LOW0, 0)}
    moves2 = {
        -2: (0, zc // 2, 7), -1: (0, zc // 2, 5), 0: (0, zc // 2, 3), 1: (0, zc // 2, 1), 2: (zc // 2 - 1, 1, 0),
    }

    order1 = [
        (slot, dz, h) for h in range(gy_n // 2) for slot, dz in ((2, 0), (0, 1), (1, -1)) if dz != 0 or h != 0
    ]

    def gather():
        sibling = gy + 1 - 2 * lax.rem(gy, 2)

        def blocks(act):
            for slot, dz in enumerate((1, -1, 0)):
                for h in range(gy_n // 2):
                    if dz == 0 and h == 0:
                        continue
                    act(slot, dz, h)

        def when_there(dz, go):
            if dz == 0:
                go()
            else:
                pl.when(there(dz))(go)

        def direct(slot, dz, h, owner):
            first, n, to = moves1[dz]
            g = lax.rem(gy + 2 * h, gy_n)
            return pltpu.make_async_remote_copy(
                src_ref=mine.at[pl.ds(first, n)],
                dst_ref=got.at[g if owner else gy, pl.ds(to, n)],
                send_sem=s1.at[slot, h],
                recv_sem=r1.at[slot, g if owner else gy],
                device_id=(gz - dz if owner else gz + dz, g),
                device_id_type=MESH,
            )

        def relay(slot, dz, h, owner):
            _, n, to = moves1[dz]
            g = lax.rem((sibling if owner else gy) + 2 * h, gy_n)
            place = got.at[g, pl.ds(to, n)]
            return pltpu.make_async_remote_copy(
                src_ref=mine if dz == 0 and h == 0 else place,
                dst_ref=place,
                send_sem=s4.at[slot, h],
                recv_sem=r1.at[slot, g],
                device_id=(gz, sibling),
                device_id_type=MESH,
            )

        blocks(lambda slot, dz, h: when_there(dz, lambda: direct(slot, dz, h, False).start()))
        relay(2, 0, 0, False).start()

        def forward(slot, dz, h):
            def go():
                direct(slot, dz, h, True).wait_recv()
                relay(slot, dz, h, False).start()

            when_there(-dz, go)

        for slot, dz, h in order1:
            forward(slot, dz, h)
        relay(2, 0, 0, True).wait_recv()
        for slot, dz, h in order1:
            when_there(-dz, lambda: relay(slot, dz, h, True).wait_recv())
        relay(2, 0, 0, False).wait_send()
        for slot, dz, h in order1:
            when_there(-dz, lambda: relay(slot, dz, h, False).wait_send())
        blocks(lambda slot, dz, h: when_there(dz, lambda: direct(slot, dz, h, False).wait_send()))

    def exchange(moves, source, target, ssem, rsem):
        sends, receives = [], []
        for slot, (dz, (first, n, to)) in enumerate(moves.items()):
            for dg in range(gy_n):
                if dz == 0 and dg == 0:
                    continue
                g = lax.rem(gy + dg, gy_n)
                send = pltpu.make_async_remote_copy(
                    src_ref=source.at[pl.ds(first, n)],
                    dst_ref=target.at[gy, pl.ds(to, n)],
                    send_sem=ssem.at[slot, dg],
                    recv_sem=rsem.at[slot, gy],
                    device_id=(gz + dz, g),
                    device_id_type=MESH,
                )
                receive = pltpu.make_async_remote_copy(
                    src_ref=source.at[pl.ds(first, n)],
                    dst_ref=target.at[g, pl.ds(to, n)],
                    send_sem=ssem.at[slot, dg],
                    recv_sem=rsem.at[slot, g],
                    device_id=(gz + dz, g),
                    device_id_type=MESH,
                )
                sends.append((dz, send))
                receives.append((-dz, receive))

        def each(items, act):
            for dz in sorted(moves, key=lambda d: -abs(d)):
                group = [item for at, item in items if at == dz]

                def go(group=group):
                    for item in group:
                        act(item)

                if dz == 0:
                    go()
                else:
                    pl.when(there(dz))(go)

        each(sends, lambda c: c.start())
        return lambda: (each(receives, lambda c: c.wait_recv()), each(sends, lambda c: c.wait_send()))

    pl.semaphore_wait(barrier, count)
    gather()

    for q in range(WINDOW):
        for k, (yp, xp) in enumerate(YX):
            for g in range(gy_n):
                f[q % 2][yp, xp, q // 2, g * y2 : (g + 1) * y2, :] = got[g, q, k * y2 : (k + 1) * y2, :]

    run0(v, f, z0, z_count, 0, 0, EVENS, PHASE_A, 0)
    run0(v, f, z0, z_count, 1, 0, ODDS, PHASE_B, 1)
    run0(v, f, z0, z_count, 0, 1, EVENS - 1, PHASE_C, 2)

    own = LOW0 // 2
    here, below, above = pl.ds(own, zc), pl.ds(own - 1, zc), pl.ds(own, zc)
    s = [[ve[yp, xp, here] + vo[yp, xp, below] + vo[yp, xp, above] for xp in (0, 1)] for yp in (0, 1)]
    tall = [s[0][xp] + pair_sum(s[1][xp], 0, 1) for xp in (0, 1)]
    dbuf[...] = fe[0, 0, here] - (27.0 * ve[0, 0, here] - (tall[0] + pair_sum(tall[1], 0, 2)))
    for z in range(zc):
        for yp in (0, 1):
            at = ((z % 2) * 2 + yp) * yc
            cmine[z // 2, at : at + yc, :] = dbuf[z, pl.ds(gy * y2 + yp, yc, stride=2), :]
    cgot[gy, pl.ds(3, zc // 2)] = cmine[...]
    for edge, low, n in ((0, 0, 3), (1, 0, 1), (gz_n - 2, 7, 2), (gz_n - 1, 5, 4)):

        @pl.when(gz == edge)
        def _(low=low, n=n):
            cgot[:, low : low + n] = jnp.zeros((gy_n, n) + cgot.shape[2:], F32)

    exchange(moves2, cmine, cgot, s2, r2)()

    for zp in (0, 1):
        for yp in (0, 1):
            at = (zp * 2 + yp) * yc
            for g in range(gy_n):
                f1[zp, yp, :, g * yc : (g + 1) * yc, :] = cgot[g, :, at : at + yc, :]

    c0, c_count = gz * zc, gz_n * zc
    run1(v1, f1, c0, c_count, 0, 0, EVENS, PHASE_A, 0)
    run1(v1, f1, c0, c_count, 1, 0, ODDS, PHASE_B, 1)
    run1(v1, f1, c0, c_count, 0, 1, EVENS - 1, PHASE_C, 2)

    f2 = []
    for i in range(1, EVENS - 1):
        s = [v1e[yp, pl.ds(i, 1)] + v1o[yp, pl.ds(i - 1, 1)] + v1o[yp, pl.ds(i, 1)] for yp in (0, 1)]
        tall = s[0] + pair_sum(s[1], 0, 1)
        f2.append(f1[0, 0, pl.ds(i, 1)] - (27.0 * v1e[0, pl.ds(i, 1)] - (tall + both_sides(tall, 2, 1))))
    q0, q_count = gz * (zc // 2), gz_n * (zc // 2)
    f2e, f2o = f2[0::2], f2[1::2]
    scale2 = [scale_rows(f2[0].shape, q0 - LOW2 + i, q_count) for i in range(7)]
    even2 = [phase2(None, f2e[k], scale2[2 * k], PHASE_A) for k in range(4)]
    odd2 = [phase2(None, f2o[k] + box2(even2[k] + even2[k + 1]), scale2[2 * k + 1], PHASE_B) for k in range(3)]
    for k in (1, 2):
        even2[k] = phase2(even2[k], f2e[k] + box2(odd2[k - 1] + odd2[k]), scale2[2 * k], PHASE_C)
    v2 = [odd2[0], even2[1], odd2[1], even2[2], odd2[2]]
    in_lane = lax.broadcasted_iota(jnp.int32, v2[0].shape, 2) % 2 == 0
    for k in range(5):
        v1e[0, pl.ds(2 + k, 1)] = v1e[0, pl.ds(2 + k, 1)] + jnp.where(in_lane, v2[k], 0.0)

    run1(v1, f1, c0, c_count, 0, 2, 7, PHASE_A, 2)
    run1(v1, f1, c0, c_count, 1, 2, 6, PHASE_B, 2)
    run1(v1, f1, c0, c_count, 0, 3, 6, PHASE_C, 2)

    half = v1e.shape[2]
    for c in range(-1, 6):
        odd = c % 2
        i = (c + LOW1 - odd) // 2
        for yp in (0, 1):
            vc[c + 1, pl.ds(yp, half, stride=2), :] = v1[odd][yp, i]
    ve[0, 0, pl.ds(1, 7)] = ve[0, 0, pl.ds(1, 7)] + vc[...]

    run0(v, f, z0, z_count, 0, 1, 8, PHASE_A, 2)
    run0(v, f, z0, z_count, 1, 1, 7, PHASE_B, 2)
    run0(v, f, z0, z_count, 0, 2, 7, PHASE_C, 2)

    numer = denom = None
    for odd in (0, 1):
        for k in range(zc):
            i = own + k
            here, below, above = pl.ds(i, 1), pl.ds(i - 1 + odd, 1), pl.ds(i + odd, 1)
            p = [[v[odd][yp, xp, here] for xp in (0, 1)] for yp in (0, 1)]
            s = [[p[yp][xp] + v[1 - odd][yp, xp, below] + v[1 - odd][yp, xp, above] for xp in (0, 1)] for yp in (0, 1)]
            b = box0(s)
            for yp, xp in YX:
                image = 27.0 * p[yp][xp] - b[yp][xp]
                numer = add(numer, f[odd][yp, xp, here] * p[yp][xp])
                denom = add(denom, p[yp][xp] * image)
                parity_at = k * 2 + odd
                nat[yp, xp, pl.ds(parity_at, 1)] = image
    rows = numer.shape[1]
    for j, total in enumerate((numer, denom)):
        acc = None
        for r in range(0, rows, 8):
            acc = add(acc, total[0, r : r + 8, :])
        part[pl.ds(j, 1), :] = jnp.sum(acc, axis=0, keepdims=True)

    sends, receives = [], []
    for d in range(1, gz_n):
        to = lax.rem(gz + d, gz_n)
        sends.append(pltpu.make_async_remote_copy(
            src_ref=part, dst_ref=parts.at[gz], send_sem=s3.at[d], recv_sem=r3.at[gz],
            device_id=(to, gy), device_id_type=MESH,
        ))
        receives.append(pltpu.make_async_remote_copy(
            src_ref=part, dst_ref=parts.at[to], send_sem=s3.at[d], recv_sem=r3.at[to],
            device_id=(to, gy), device_id_type=MESH,
        ))
    for c in sends:
        c.start()
    parts[gz] = part[...]

    back = permutation(nx, True)
    for which, out in ((0, sol_ref), (1, res_ref)):
        for z in range(zl):
            for yp, xp in YX:
                if which == 0:
                    row = v[z % 2][yp, xp, own + z // 2, pl.ds(gy * y2, y2), :]
                else:
                    row = nat[yp, xp, z, pl.ds(gy * y2, y2), :]
                flat[xp, pl.ds(z * yl + yp, y2, stride=2), :] = row
        out[...] = jnp.dot(
            jnp.concatenate([flat[0], flat[1]], axis=1), back, precision=lax.Precision.HIGHEST, preferred_element_type=F32
        ).reshape(zl, yl, nx)

    for c in receives:
        c.wait_recv()
    for c in sends:
        c.wait_send()
    sums = parts[0]
    for d in range(1, gz_n):
        sums = sums + parts[d]
    alpha = jnp.sum(sums[0:1], axis=1, keepdims=True) / jnp.sum(sums[1:2], axis=1, keepdims=True)
    alpha = alpha.reshape(1, 1, 1)
    sol_ref[...] = sol_ref[...] * alpha
    res_ref[...] = rhs_ref[...] - res_ref[...] * alpha


def solution(mesh):
    gz_n, gy_n = mesh.shape["gz"], mesh.shape["gy"]

    def body(rhs):
        zl, yl, nx = rhs.shape
        y2, x2 = yl // 2, nx // 2
        y_half = gy_n * y2
        zc, yc = zl // 2, y2 // 2
        vmem = lambda *shape: pltpu.VMEM(shape, F32)
        dma = lambda *shape: pltpu.SemaphoreType.DMA(shape)
        return pl.pallas_call(
            functools.partial(kernel, gz_n, gy_n),
            out_shape=[jax.ShapeDtypeStruct(rhs.shape, F32)] * 2,
            in_specs=[pl.BlockSpec(memory_space=pl.ANY)],
            out_specs=[pl.BlockSpec(memory_space=pltpu.VMEM)] * 2,
            scratch_shapes=[
                vmem(2, zl * yl, x2),
                vmem(zl, 4 * y2, x2),
                vmem(gy_n, WINDOW, 4 * y2, x2),
                vmem(2, 2, EVENS, y_half, x2),
                vmem(2, 2, ODDS, y_half, x2),
                vmem(2, 2, EVENS, y_half, x2),
                vmem(2, 2, ODDS, y_half, x2),
                vmem(zc, y_half, x2),
                vmem(zc // 2, 4 * yc, x2),
                vmem(gy_n, 9, 4 * yc, x2),
                vmem(2, 2, 9, gy_n * yc, x2),
                vmem(2, EVENS, gy_n * yc, x2),
                vmem(2, ODDS, gy_n * yc, x2),
                vmem(7, y_half, x2),
                vmem(2, x2),
                vmem(gz_n, 2, x2),
                vmem(2, 2, zl, y_half, x2),
                dma(3, gy_n), dma(3, gy_n), dma(5, gy_n), dma(5, gy_n), dma(gz_n), dma(gz_n), dma(3, gy_n),
                vmem(zl, yl, nx), pltpu.SemaphoreType.DMA,
            ],
            compiler_params=pltpu.CompilerParams(has_side_effects=True, collective_id=0),
        )(rhs)

    return jax.shard_map(
        lambda rhs: tuple(body(rhs)),
        mesh=mesh,
        in_specs=(P("gz", "gy", None),),
        out_specs=(P("gz", "gy", None), P("gz", "gy", None)),
        check_vma=False,
    )
```

profile of v0, /device:TPU:0, one launch (start us, length us, event | category | flops | bytes accessed | tf_op | source)
XLA Modules:
  0.0 29.6 jit_solution(2518370971391067673)
XLA Ops:
  0.6 26.8 %shard_map.30 = (f32[8,8,256]{2,1,0:T(8,128)}, f32[8,8,256]{2,1,0:T(8,128)}) custom-call(f32[8,8,256]{2,1,0:T(8,128)} %rhs_hbm.1), custom_call_target="tpu_custom_call" | custom-call | tf_op jit(solution)/shard_map/pallas_call | solution.py:471
  27.5 0.0 copy-start
  27.5 1.5 %copy.5 = f32[8,8,256]{2,1,0:T(8,128)} copy(f32[8,8,256]{2,1,0:T(8,128)} %get-tuple-element.4) | data formatting | bytes 131072
  29.0 0.0 copy-done
  29.0 0.6 %copy.6 = f32[8,8,256]{2,1,0:T(8,128)} copy(f32[8,8,256]{2,1,0:T(8,128)S(1)} %copy-done) | data formatting | bytes 131072
Async XLA Ops:
  27.5 1.5 %copy-start = (f32[8,8,256]{2,1,0:T(8,128)S(1)}, f32[8,8,256]{2,1,0:T(8,128)}, u32[]{:S(2)}) copy-start(f32[8,8,256]{2,1,0:T(8,128)} %get-tuple-element.5) | copy-start | bytes 196612
where the time goes:
time: 29.8 us; the launch traced here: 29.6 us
  Pallas kernels  26.8 us (90%)
  local copies, waits for them, and re-layouts  2.14 us (7%)
  between operations  0.65 us (2%)
    pallas_call x1, Pallas kernels, body(): pl.pallas_call(functools.partial(kernel, gz_n, gy_n), out_shape=[jax.Shap...  26.8 us
    unnamed x4, local copies, waits for them, and re-layouts  2.14 us

commit v1 on v0

--- a/solution.py
+++ b/solution.py
@@ -58,13 +58,28 @@
     return [[add(tall[yp][xp], pair_sum(tall[yp][1 - xp], xp, 2)) for xp in (0, 1)] for yp in (0, 1)]
 
 
-def phase0(v, g, scale, steps):
+def edge_twice(x, axis, width, at_end):
+    size = x.shape[axis]
+    index = lax.broadcasted_iota(jnp.int32, x.shape, axis)
+    inner = index < size - width if at_end else index >= width
+    return x * jnp.where(inner, F32(2.0), F32(1.0))
+
+
+def phase0(v, f, zs, scale, steps):
     v = [list(v[0]), list(v[1])]
     for yp, order in steps:
-        w = [pair_sum(v[1 - yp][xp], yp, 1) for xp in (0, 1)]
-        for xp in order:
-            side = pair_sum(add(w[1 - xp], v[yp][1 - xp]), xp, 2)
-            v[yp][xp] = add(g[yp][xp], w[xp], side) * scale
+        w = [add(zs[yp][xp], pair_sum(add(zs[1 - yp][xp], v[1 - yp][xp]), yp, 1)) for xp in (0, 1)]
+        a, b = order[0], order[1]
+        near, far = (1, -1) if a == 0 else (-1, 1)
+        u = add(w[b], v[yp][b])
+        h = add(f[yp][a], w[a])
+        q = add(w[a], h * scale)
+        u_near = shift(u, 2, near)
+        v[yp][a] = add(h, u, u_near) * scale
+        twice = None if u is None else add(edge_twice(u, 2, 1, a == 0), u_near, shift(u, 2, far)) * scale
+        v[yp][b] = add(f[yp][b], w[b], q, shift(q, 2, far), twice) * scale
+        if len(order) == 3:
+            v[yp][a] = add(h, pair_sum(add(w[b], v[yp][b]), a, 2)) * scale
     return v
 
 
@@ -73,34 +88,36 @@
     return [add(t, both_sides(t, 2, 1)) for t in tall]
 
 
-def phase1(v, g, scale, steps):
+def line_pair(v, g, w, scale, parity, order, step):
+    a, b = order[0], order[1]
+    first = parity == a
+    h = add(g, w)
+    u = add(w, v)
+    m = jnp.where(first, add(w, h * scale), 0.0 if u is None else u)
+    second = add(edge_twice(m, 2, step, b == 1), both_sides(m, 2, 2 * step)) * jnp.where(first, F32(0.0), scale)
+    new = add(h, both_sides(m, 2, step), second) * scale
+    if len(order) == 3:
+        new = jnp.where(first, add(h, both_sides(add(w, new), 2, step)) * scale, new)
+    return new
+
+
+def phase1(v, g, zs, scale, steps):
     v = list(v)
-    shape = scale.shape
-    parity = lax.broadcasted_iota(jnp.int32, shape, 2) % 2
+    parity = lax.broadcasted_iota(jnp.int32, scale.shape, 2) % 2
     for yp, order in steps:
-        w = pair_sum(v[1 - yp], yp, 1)
-        for xp in order:
-            new = add(g[yp], w, both_sides(add(w, v[yp]), 2, 1)) * scale
-            v[yp] = jnp.where(parity == xp, new, 0.0 if v[yp] is None else v[yp])
+        w = add(zs[yp], pair_sum(add(zs[1 - yp], v[1 - yp]), yp, 1))
+        v[yp] = line_pair(v[yp], g[yp], w, scale, parity, order, 1)
     return v
 
 
-def box2(s):
-    if s is None:
-        return None
-    tall = add(s, both_sides(s, 1, 1))
-    return add(tall, both_sides(tall, 2, 2))
-
-
-def phase2(v, g, scale, steps):
+def phase2(v, g, zs, scale, steps):
     shape = scale.shape
     y_par = lax.broadcasted_iota(jnp.int32, shape, 1) % 2
     x_par = (lax.broadcasted_iota(jnp.int32, shape, 2) // 2) % 2
     for yp, order in steps:
-        w = both_sides(v, 1, 1)
-        for xp in order:
-            new = add(g, w, both_sides(add(w, v), 2, 2)) * scale
-            v = jnp.where((y_par == yp) & (x_par == xp), new, 0.0 if v is None else v)
+        w = add(zs, both_sides(add(zs, v), 1, 1))
+        new = line_pair(v, g, w, scale, x_par, order, 2)
+        v = jnp.where(y_par == yp, new, 0.0 if v is None else v)
     return v
 
 
@@ -110,6 +127,9 @@
 
 
 YX = [(0, 0), (0, 1), (1, 0), (1, 1)]
+
+
+NONE = [[None, None], [None, None]]
 
 
 def run0(v, f, z0, z_count, odd, low, high, steps, fresh):
@@ -117,15 +137,13 @@
         here = pl.ds(at, n)
         below, above = (pl.ds(at, n), pl.ds(at + 1, n)) if odd else (pl.ds(at - 1, n), pl.ds(at, n))
         rhs = [[f[odd][yp, xp, here] for xp in (0, 1)] for yp in (0, 1)]
-        shape = rhs[0][0].shape
-        scale = scale_rows(shape, z0 + 2 * at - LOW0 + odd, z_count)
-        g = rhs
+        scale = scale_rows(rhs[0][0].shape, z0 + 2 * at - LOW0 + odd, z_count)
+        zs, old = NONE, NONE
         if fresh > 0:
-            s = [[v[1 - odd][yp, xp, below] + v[1 - odd][yp, xp, above] for xp in (0, 1)] for yp in (0, 1)]
-            b = box0(s)
-            g = [[rhs[yp][xp] + b[yp][xp] for xp in (0, 1)] for yp in (0, 1)]
-        old = [[v[odd][yp, xp, here] if fresh > 1 else None for xp in (0, 1)] for yp in (0, 1)]
-        new = phase0(old, g, scale, steps)
+            zs = [[v[1 - odd][yp, xp, below] + v[1 - odd][yp, xp, above] for xp in (0, 1)] for yp in (0, 1)]
+        if fresh > 1:
+            old = [[v[odd][yp, xp, here] for xp in (0, 1)] for yp in (0, 1)]
+        new = phase0(old, rhs, zs, scale, steps)
         for yp, xp in YX:
             v[odd][yp, xp, here] = new[yp][xp]
 
@@ -134,13 +152,14 @@
     for at, n in chunks(low, high, CHUNK1):
         here = pl.ds(at, n)
         below, above = (pl.ds(at, n), pl.ds(at + 1, n)) if odd else (pl.ds(at - 1, n), pl.ds(at, n))
-        g = [f[odd, yp, here] for yp in (0, 1)]
+        g = [f[here, odd, yp] for yp in (0, 1)]
         scale = scale_rows(g[0].shape, z0 + 2 * at - LOW1 + odd, z_count)
+        zs, old = NONE[0], NONE[0]
         if fresh > 0:
-            b = box1([v[1 - odd][yp, below] + v[1 - odd][yp, above] for yp in (0, 1)])
-            g = [g[yp] + b[yp] for yp in (0, 1)]
-        old = [v[odd][yp, here] if fresh > 1 else None for yp in (0, 1)]
-        new = phase1(old, g, scale, steps)
+            zs = [v[1 - odd][yp, below] + v[1 - odd][yp, above] for yp in (0, 1)]
+        if fresh > 1:
+            old = [v[odd][yp, here] for yp in (0, 1)]
+        new = phase1(old, g, zs, scale, steps)
         for yp in (0, 1):
             v[odd][yp, here] = new[yp]
 
@@ -155,8 +174,8 @@
 
 def kernel(
     gz_n, gy_n, rhs_hbm, sol_ref, res_ref,
-    flat, mine, got, fe, fo, ve, vo, dbuf, cmine, cgot, f1, v1e, v1o, vc, part, parts, nat,
-    s1, r1, s2, r2, s3, r3, s4, rhs_ref, s5,
+    flat, mine, got, fe, fo, ve, vo, dbuf, f1, v1e, v1o, vc, part, parts, nat,
+    ssem, r1, r2, r3, rhs_ref, s5, token,
 ):
     gz, gy = lax.axis_index("gz"), lax.axis_index("gy")
     zl, yl, nx = rhs_ref.shape
@@ -169,24 +188,30 @@
     z0 = gz * zl
     f, v = (fe, fo), (ve, vo)
     v1 = (v1e, v1o)
+    halves = gy_n // 2
+    sibling = gy + 1 - 2 * lax.rem(gy, 2)
 
     def there(dz):
         return (gz + dz >= 0) & (gz + dz < gz_n)
 
+    def when_there(dz, go):
+        if dz == 0:
+            go()
+        else:
+            pl.when(there(dz))(go)
+
     barrier = pltpu.get_barrier_semaphore()
     count = jnp.int32(0)
-    for dz in range(1 - gz_n, gz_n):
-        for dg in range(gy_n if abs(dz) <= 2 else 1):
-            if dz == 0 and dg == 0:
-                continue
-
-            @pl.when(there(dz))
-            def _(dz=dz, dg=dg):
-                pl.semaphore_signal(
-                    barrier, inc=1, device_id=(gz + dz, lax.rem(gy + dg, gy_n)), device_id_type=MESH
-                )
-
-            count = count + there(dz).astype(jnp.int32)
+    greet = [(0, dg) for dg in range(1, gy_n)] + [(dz, 2 * h) for dz in (-1, 1) for h in range(halves)] + [(-2, 0), (2, 0)]
+    for dz, dg in greet:
+
+        def go(dz=dz, dg=dg):
+            pl.semaphore_signal(
+                barrier, inc=1, device_id=(gz + dz, lax.rem(gy + dg, gy_n)), device_id_type=MESH
+            )
+
+        when_there(dz, go)
+        count = count + (1 if dz == 0 else there(dz).astype(jnp.int32))
 
     fetch.wait()
     split = jnp.dot(
@@ -211,29 +236,30 @@
 
     high = WINDOW - LOW0 - zl
     moves1 = {-1: (0, high, LOW0 + zl), 0: (0, zl, LOW0), 1: (zl - LOW0, LOW0, 0)}
-    moves2 = {
-        -2: (0, zc // 2, 7), -1: (0, zc // 2, 5), 0: (0, zc // 2, 3), 1: (0, zc // 2, 1), 2: (zc // 2 - 1, 1, 0),
-    }
+    moves2 = {-2: (0, zc // 2, 7), -1: (0, zc // 2, 5), 1: (0, zc // 2, 1), 2: (zc // 2 - 1, 1, 0)}
 
     order1 = [
-        (slot, dz, h) for h in range(gy_n // 2) for slot, dz in ((2, 0), (0, 1), (1, -1)) if dz != 0 or h != 0
+        (slot, dz, h) for h in range(halves) for slot, dz in ((2, 0), (0, 1), (1, -1)) if dz != 0 or h != 0
     ]
 
+    def pass_token(round_):
+        reach = 2 << round_
+        for dz in (-reach, reach):
+            when_there(dz, lambda dz=dz: pl.semaphore_signal(
+                token.at[round_], inc=1, device_id=(gz + dz, gy), device_id_type=MESH
+            ))
+
+    def take_token(round_):
+        reach = 2 << round_
+        pl.semaphore_wait(token.at[round_], there(-reach).astype(jnp.int32) + there(reach).astype(jnp.int32))
+
     def gather():
-        sibling = gy + 1 - 2 * lax.rem(gy, 2)
-
         def blocks(act):
             for slot, dz in enumerate((1, -1, 0)):
-                for h in range(gy_n // 2):
+                for h in range(halves):
                     if dz == 0 and h == 0:
                         continue
                     act(slot, dz, h)
-
-        def when_there(dz, go):
-            if dz == 0:
-                go()
-            else:
-                pl.when(there(dz))(go)
 
         def direct(slot, dz, h, owner):
             first, n, to = moves1[dz]
@@ -241,7 +267,7 @@
             return pltpu.make_async_remote_copy(
                 src_ref=mine.at[pl.ds(first, n)],
                 dst_ref=got.at[g if owner else gy, pl.ds(to, n)],
-                send_sem=s1.at[slot, h],
+                send_sem=ssem.at[slot * halves + h],
                 recv_sem=r1.at[slot, g if owner else gy],
                 device_id=(gz - dz if owner else gz + dz, g),
                 device_id_type=MESH,
@@ -254,7 +280,7 @@
             return pltpu.make_async_remote_copy(
                 src_ref=mine if dz == 0 and h == 0 else place,
                 dst_ref=place,
-                send_sem=s4.at[slot, h],
+                send_sem=ssem.at[(3 + slot) * halves + h],
                 recv_sem=r1.at[slot, g],
                 device_id=(gz, sibling),
                 device_id_type=MESH,
@@ -272,6 +298,10 @@
 
         for slot, dz, h in order1:
             forward(slot, dz, h)
+        for r in range(min(rounds, 1)):
+            take_token(r)
+            if r + 1 < rounds:
+                pass_token(r + 1)
         relay(2, 0, 0, True).wait_recv()
         for slot, dz, h in order1:
             when_there(-dz, lambda: relay(slot, dz, h, True).wait_recv())
@@ -280,49 +310,10 @@
             when_there(-dz, lambda: relay(slot, dz, h, False).wait_send())
         blocks(lambda slot, dz, h: when_there(dz, lambda: direct(slot, dz, h, False).wait_send()))
 
-    def exchange(moves, source, target, ssem, rsem):
-        sends, receives = [], []
-        for slot, (dz, (first, n, to)) in enumerate(moves.items()):
-            for dg in range(gy_n):
-                if dz == 0 and dg == 0:
-                    continue
-                g = lax.rem(gy + dg, gy_n)
-                send = pltpu.make_async_remote_copy(
-                    src_ref=source.at[pl.ds(first, n)],
-                    dst_ref=target.at[gy, pl.ds(to, n)],
-                    send_sem=ssem.at[slot, dg],
-                    recv_sem=rsem.at[slot, gy],
-                    device_id=(gz + dz, g),
-                    device_id_type=MESH,
-                )
-                receive = pltpu.make_async_remote_copy(
-                    src_ref=source.at[pl.ds(first, n)],
-                    dst_ref=target.at[g, pl.ds(to, n)],
-                    send_sem=ssem.at[slot, dg],
-                    recv_sem=rsem.at[slot, g],
-                    device_id=(gz + dz, g),
-                    device_id_type=MESH,
-                )
-                sends.append((dz, send))
-                receives.append((-dz, receive))
-
-        def each(items, act):
-            for dz in sorted(moves, key=lambda d: -abs(d)):
-                group = [item for at, item in items if at == dz]
-
-                def go(group=group):
-                    for item in group:
-                        act(item)
-
-                if dz == 0:
-                    go()
-                else:
-                    pl.when(there(dz))(go)
-
-        each(sends, lambda c: c.start())
-        return lambda: (each(receives, lambda c: c.wait_recv()), each(sends, lambda c: c.wait_send()))
-
+    rounds = max(gz_n - 2, 1).bit_length() - 1
     pl.semaphore_wait(barrier, count)
+    if rounds > 0:
+        pass_token(0)
     gather()
 
     for q in range(WINDOW):
@@ -339,24 +330,36 @@
     s = [[ve[yp, xp, here] + vo[yp, xp, below] + vo[yp, xp, above] for xp in (0, 1)] for yp in (0, 1)]
     tall = [s[0][xp] + pair_sum(s[1][xp], 0, 1) for xp in (0, 1)]
     dbuf[...] = fe[0, 0, here] - (27.0 * ve[0, 0, here] - (tall[0] + pair_sum(tall[1], 0, 2)))
+    half = gy_n * yc
     for z in range(zc):
         for yp in (0, 1):
-            at = ((z % 2) * 2 + yp) * yc
-            cmine[z // 2, at : at + yc, :] = dbuf[z, pl.ds(gy * y2 + yp, yc, stride=2), :]
-    cgot[gy, pl.ds(3, zc // 2)] = cmine[...]
+            f1[3 + z // 2, z % 2, yp] = dbuf[z, pl.ds(yp, half, stride=2), :]
     for edge, low, n in ((0, 0, 3), (1, 0, 1), (gz_n - 2, 7, 2), (gz_n - 1, 5, 4)):
 
         @pl.when(gz == edge)
         def _(low=low, n=n):
-            cgot[:, low : low + n] = jnp.zeros((gy_n, n) + cgot.shape[2:], F32)
-
-    exchange(moves2, cmine, cgot, s2, r2)()
-
-    for zp in (0, 1):
-        for yp in (0, 1):
-            at = (zp * 2 + yp) * yc
-            for g in range(gy_n):
-                f1[zp, yp, :, g * yc : (g + 1) * yc, :] = cgot[g, :, at : at + yc, :]
+            f1[low : low + n] = jnp.zeros((n,) + f1.shape[1:], F32)
+
+    def near(slot, dz):
+        first, n, to = moves2[dz]
+        return pltpu.make_async_remote_copy(
+            src_ref=f1.at[pl.ds(3 + first, n)], dst_ref=f1.at[pl.ds(to, n)],
+            send_sem=ssem.at[slot], recv_sem=r2.at[slot],
+            device_id=(gz + dz, gy), device_id_type=MESH,
+        )
+
+    far_first = sorted(moves2, key=lambda d: -abs(d))
+    for slot, dz in enumerate(far_first):
+        when_there(dz, lambda: near(slot, dz).start())
+    for slot, dz in enumerate(far_first):
+        when_there(-dz, lambda: near(slot, dz).wait_recv())
+    for slot, dz in enumerate(far_first):
+        when_there(dz, lambda: near(slot, dz).wait_send())
+
+    for r in range(1, rounds):
+        take_token(r)
+        if r + 1 < rounds:
+            pass_token(r + 1)
 
     c0, c_count = gz * zc, gz_n * zc
     run1(v1, f1, c0, c_count, 0, 0, EVENS, PHASE_A, 0)
@@ -367,14 +370,14 @@
     for i in range(1, EVENS - 1):
         s = [v1e[yp, pl.ds(i, 1)] + v1o[yp, pl.ds(i - 1, 1)] + v1o[yp, pl.ds(i, 1)] for yp in (0, 1)]
         tall = s[0] + pair_sum(s[1], 0, 1)
-        f2.append(f1[0, 0, pl.ds(i, 1)] - (27.0 * v1e[0, pl.ds(i, 1)] - (tall + both_sides(tall, 2, 1))))
+        f2.append(f1[pl.ds(i, 1), 0, 0] - (27.0 * v1e[0, pl.ds(i, 1)] - (tall + both_sides(tall, 2, 1))))
     q0, q_count = gz * (zc // 2), gz_n * (zc // 2)
     f2e, f2o = f2[0::2], f2[1::2]
     scale2 = [scale_rows(f2[0].shape, q0 - LOW2 + i, q_count) for i in range(7)]
-    even2 = [phase2(None, f2e[k], scale2[2 * k], PHASE_A) for k in range(4)]
-    odd2 = [phase2(None, f2o[k] + box2(even2[k] + even2[k + 1]), scale2[2 * k + 1], PHASE_B) for k in range(3)]
+    even2 = [phase2(None, f2e[k], None, scale2[2 * k], PHASE_A) for k in range(4)]
+    odd2 = [phase2(None, f2o[k], even2[k] + even2[k + 1], scale2[2 * k + 1], PHASE_B) for k in range(3)]
     for k in (1, 2):
-        even2[k] = phase2(even2[k], f2e[k] + box2(odd2[k - 1] + odd2[k]), scale2[2 * k], PHASE_C)
+        even2[k] = phase2(even2[k], f2e[k], odd2[k - 1] + odd2[k], scale2[2 * k], PHASE_C)
     v2 = [odd2[0], even2[1], odd2[1], even2[2], odd2[2]]
     in_lane = lax.broadcasted_iota(jnp.int32, v2[0].shape, 2) % 2 == 0
     for k in range(5):
@@ -384,7 +387,6 @@
     run1(v1, f1, c0, c_count, 1, 2, 6, PHASE_B, 2)
     run1(v1, f1, c0, c_count, 0, 3, 6, PHASE_C, 2)
 
-    half = v1e.shape[2]
     for c in range(-1, 6):
         odd = c % 2
         i = (c + LOW1 - odd) // 2
@@ -421,11 +423,11 @@
     for d in range(1, gz_n):
         to = lax.rem(gz + d, gz_n)
         sends.append(pltpu.make_async_remote_copy(
-            src_ref=part, dst_ref=parts.at[gz], send_sem=s3.at[d], recv_sem=r3.at[gz],
+            src_ref=part, dst_ref=parts.at[gz], send_sem=ssem.at[d - 1], recv_sem=r3.at[gz],
             device_id=(to, gy), device_id_type=MESH,
         ))
         receives.append(pltpu.make_async_remote_copy(
-            src_ref=part, dst_ref=parts.at[to], send_sem=s3.at[d], recv_sem=r3.at[to],
+            src_ref=part, dst_ref=parts.at[to], send_sem=ssem.at[d - 1], recv_sem=r3.at[to],
             device_id=(to, gy), device_id_type=MESH,
         ))
     for c in sends:
@@ -470,7 +472,7 @@
         dma = lambda *shape: pltpu.SemaphoreType.DMA(shape)
         return pl.pallas_call(
             functools.partial(kernel, gz_n, gy_n),
-            out_shape=[jax.ShapeDtypeStruct(rhs.shape, F32)] * 2,
+            out_shape=[vmem(*rhs.shape)] * 2,
             in_specs=[pl.BlockSpec(memory_space=pl.ANY)],
             out_specs=[pl.BlockSpec(memory_space=pltpu.VMEM)] * 2,
             scratch_shapes=[
@@ -482,17 +484,16 @@
                 vmem(2, 2, EVENS, y_half, x2),
                 vmem(2, 2, ODDS, y_half, x2),
                 vmem(zc, y_half, x2),
-                vmem(zc // 2, 4 * yc, x2),
-                vmem(gy_n, 9, 4 * yc, x2),
-                vmem(2, 2, 9, gy_n * yc, x2),
+                vmem(9, 2, 2, gy_n * yc, x2),
                 vmem(2, EVENS, gy_n * yc, x2),
                 vmem(2, ODDS, gy_n * yc, x2),
                 vmem(7, y_half, x2),
                 vmem(2, x2),
                 vmem(gz_n, 2, x2),
                 vmem(2, 2, zl, y_half, x2),
-                dma(3, gy_n), dma(3, gy_n), dma(5, gy_n), dma(5, gy_n), dma(gz_n), dma(gz_n), dma(3, gy_n),
+                dma(max(6 * (gy_n // 2), gz_n)), dma(3, gy_n), dma(4), dma(gz_n),
                 vmem(zl, yl, nx), pltpu.SemaphoreType.DMA,
+                pltpu.SemaphoreType.REGULAR((max(1, max(gz_n - 2, 1).bit_length() - 1),)),
             ],
             compiler_params=pltpu.CompilerParams(has_side_effects=True, collective_id=0),
         )(rhs)

time: 29.8 us -> 25.4 us (0.85)
  Pallas kernels: 26.8 us -> 23.4 us
  local copies, waits for them, and re-layouts: 2.14 us -> 1.26 us
    pallas_call x1, Pallas kernels: 26.8 us -> 23.4 us  [body(): pl.pallas_call(functools.partial(kernel, gz_n, gy_n), out_shape=[vmem(*rh...]
    unnamed x4 -> x2, local copies, waits for them, and re-layouts: 2.14 us -> 1.26 us
where the time goes in v1:
time: 25.4 us; the launch traced here: 25.3 us
  Pallas kernels  23.4 us (92%)
  local copies, waits for them, and re-layouts  1.26 us (5%)
  between operations  0.64 us (3%)
    pallas_call x1, Pallas kernels, body(): pl.pallas_call(functools.partial(kernel, gz_n, gy_n), out_shape=[vmem(*rh...  23.4 us
    unnamed x2, local copies, waits for them, and re-layouts  1.26 us

profile of v1, /device:TPU:0, one launch (start us, length us, event | category | flops | bytes accessed | tf_op | source)
XLA Modules:
  0.0 25.3 jit_solution(8363163478595386661)
XLA Ops:
  0.6 23.4 %shard_map.30 = (f32[8,8,256]{2,1,0:T(8,128)S(1)}, f32[8,8,256]{2,1,0:T(8,128)S(1)}) custom-call(f32[8,8,256]{2,1,0:T(8,128)} %rhs_hbm.1), custom_call_target="tpu_custom_call" | custom-call | tf_op jit(solution)/shard_map/pallas_call | solution.py:473
  24.0 0.6 %copy.5 = f32[8,8,256]{2,1,0:T(8,128)} copy(f32[8,8,256]{2,1,0:T(8,128)S(1)} %get-tuple-element.2) | data formatting | bytes 131072
  24.7 0.6 %copy.6 = f32[8,8,256]{2,1,0:T(8,128)} copy(f32[8,8,256]{2,1,0:T(8,128)S(1)} %get-tuple-element.3) | data formatting | bytes 131072

commit v2 on v1

--- a/solution.py
+++ b/solution.py
@@ -172,10 +172,26 @@
     return jnp.where(tall == source, F32(1.0), F32(0.0))
 
 
+def when(condition, act):
+    @pl.when(condition)
+    def _():
+        act()
+
+
+def send_order(far, halves):
+    order = [(dz, h) for dz in (far, 0, -far) for h in reversed(range(halves))]
+    return [(dz, h) for dz, h in order if dz != 0 or h != 0]
+
+
+def receive_order(far, halves):
+    order = [(dz, h) for h in range(halves) for dz in (0, -far, far)]
+    return [(dz, h) for dz, h in order if dz != 0 or h != 0]
+
+
 def kernel(
-    gz_n, gy_n, rhs_hbm, sol_ref, res_ref,
+    gz_n, gy_n, rhs_hbm, sol_ref, res_ref, alpha_ref,
     flat, mine, got, fe, fo, ve, vo, dbuf, f1, v1e, v1o, vc, part, parts, nat,
-    ssem, r1, r2, r3, rhs_ref, s5, token,
+    ssem, r1, r2, r3, rs, rhs_ref, s5, token,
 ):
     gz, gy = lax.axis_index("gz"), lax.axis_index("gy")
     zl, yl, nx = rhs_ref.shape
@@ -198,11 +214,11 @@
         if dz == 0:
             go()
         else:
-            pl.when(there(dz))(go)
+            when(there(dz), go)
 
     barrier = pltpu.get_barrier_semaphore()
     count = jnp.int32(0)
-    greet = [(0, dg) for dg in range(1, gy_n)] + [(dz, 2 * h) for dz in (-1, 1) for h in range(halves)] + [(-2, 0), (2, 0)]
+    greet = [(dz, 2 * h) for h in reversed(range(halves)) for dz in (-1, 1)] + [(-2, 0), (2, 0)] + [(0, dg) for dg in range(1, gy_n)]
     for dz, dg in greet:
 
         def go(dz=dz, dg=dg):
@@ -214,12 +230,14 @@
         count = count + (1 if dz == 0 else there(dz).astype(jnp.int32))
 
     fetch.wait()
-    split = jnp.dot(
-        rhs_ref[...].reshape(zl * yl, nx), permutation(nx, False),
-        precision=lax.Precision.HIGHEST, preferred_element_type=F32,
-    )
+    lane = lax.broadcasted_iota(jnp.int32, (zl * yl, x2), 1)
+    source = 2 * lax.rem(lane, x2 // 2)
+    rows = rhs_ref[...].reshape(zl * yl, nx)
     for xp in (0, 1):
-        flat[xp] = split[:, xp * x2 : (xp + 1) * x2]
+        left, right = (
+            jnp.take_along_axis(rows[:, i : i + x2], source + xp, axis=1, mode="promise_in_bounds") for i in (0, x2)
+        )
+        flat[xp] = jnp.where(lane < x2 // 2, left, right)
     for z in range(zl):
         for yp, xp in YX:
             row = flat[xp, pl.ds(z * yl + yp, y2, stride=2), :]
@@ -237,10 +255,6 @@
     high = WINDOW - LOW0 - zl
     moves1 = {-1: (0, high, LOW0 + zl), 0: (0, zl, LOW0), 1: (zl - LOW0, LOW0, 0)}
     moves2 = {-2: (0, zc // 2, 7), -1: (0, zc // 2, 5), 1: (0, zc // 2, 1), 2: (zc // 2 - 1, 1, 0)}
-
-    order1 = [
-        (slot, dz, h) for h in range(halves) for slot, dz in ((2, 0), (0, 1), (1, -1)) if dz != 0 or h != 0
-    ]
 
     def pass_token(round_):
         reach = 2 << round_
@@ -253,73 +267,79 @@
         reach = 2 << round_
         pl.semaphore_wait(token.at[round_], there(-reach).astype(jnp.int32) + there(reach).astype(jnp.int32))
 
+    def each_parity(index, act):
+        for parity in (0, 1):
+            when(lax.rem(index, 2) == parity, lambda parity=parity: act(parity))
+
+    def unpack(dz, g):
+        _, n, to = moves1[dz]
+        for q in range(to, to + n):
+            for k, (yp, xp) in enumerate(YX):
+                f[q % 2][yp, xp, q // 2, g * y2 : (g + 1) * y2, :] = got[g, q, k * y2 : (k + 1) * y2, :]
+
     def gather():
-        def blocks(act):
-            for slot, dz in enumerate((1, -1, 0)):
-                for h in range(halves):
-                    if dz == 0 and h == 0:
-                        continue
-                    act(slot, dz, h)
-
-        def direct(slot, dz, h, owner):
+        slots = {1: 0, -1: 1, 0: 2}
+
+        def direct(dz, h, owner):
             first, n, to = moves1[dz]
             g = lax.rem(gy + 2 * h, gy_n)
             return pltpu.make_async_remote_copy(
                 src_ref=mine.at[pl.ds(first, n)],
                 dst_ref=got.at[g if owner else gy, pl.ds(to, n)],
-                send_sem=ssem.at[slot * halves + h],
-                recv_sem=r1.at[slot, g if owner else gy],
+                send_sem=ssem.at[slots[dz] * halves + h],
+                recv_sem=r1.at[slots[dz], g if owner else gy],
                 device_id=(gz - dz if owner else gz + dz, g),
                 device_id_type=MESH,
             )
 
-        def relay(slot, dz, h, owner):
+        def relay(dz, h, owner):
             _, n, to = moves1[dz]
             g = lax.rem((sibling if owner else gy) + 2 * h, gy_n)
             place = got.at[g, pl.ds(to, n)]
             return pltpu.make_async_remote_copy(
                 src_ref=mine if dz == 0 and h == 0 else place,
                 dst_ref=place,
-                send_sem=ssem.at[(3 + slot) * halves + h],
-                recv_sem=r1.at[slot, g],
+                send_sem=ssem.at[(3 + slots[dz]) * halves + h],
+                recv_sem=r1.at[slots[dz], g],
                 device_id=(gz, sibling),
                 device_id_type=MESH,
             )
 
-        blocks(lambda slot, dz, h: when_there(dz, lambda: direct(slot, dz, h, False).start()))
-        relay(2, 0, 0, False).start()
-
-        def forward(slot, dz, h):
-            def go():
-                direct(slot, dz, h, True).wait_recv()
-                relay(slot, dz, h, False).start()
-
-            when_there(-dz, go)
-
-        for slot, dz, h in order1:
-            forward(slot, dz, h)
-        for r in range(min(rounds, 1)):
-            take_token(r)
-            if r + 1 < rounds:
-                pass_token(r + 1)
-        relay(2, 0, 0, True).wait_recv()
-        for slot, dz, h in order1:
-            when_there(-dz, lambda: relay(slot, dz, h, True).wait_recv())
-        relay(2, 0, 0, False).wait_send()
-        for slot, dz, h in order1:
-            when_there(-dz, lambda: relay(slot, dz, h, False).wait_send())
-        blocks(lambda slot, dz, h: when_there(dz, lambda: direct(slot, dz, h, False).wait_send()))
+        def sends(parity):
+            far = -1 if parity == 0 else 1
+            for dz, h in send_order(far, halves):
+                when_there(dz, lambda: direct(dz, h, False).start())
+
+        each_parity(gz, sends)
+        relay(0, 0, False).start()
+
+        def forwards(parity):
+            far = 1 if parity == 0 else -1
+            for dz, h in receive_order(far, halves):
+
+                def go():
+                    direct(dz, h, True).wait_recv()
+                    relay(dz, h, False).start()
+
+                when_there(-dz, go)
+
+        each_parity(gz, forwards)
+        if rounds > 0:
+            pass_token(0)
+        each_parity(gy, lambda parity: [unpack(dz, g) for dz in (0, 1, -1) for g in range(parity, gy_n, 2)])
+        for dz in (0, 1, -1):
+            for h in range(halves):
+                when_there(-dz, lambda: relay(dz, h, True).wait_recv())
+            each_parity(gy, lambda parity: [unpack(dz, g) for g in range(1 - parity, gy_n, 2)])
+        for dz in (0, 1, -1):
+            for h in range(halves):
+                when_there(-dz, lambda: relay(dz, h, False).wait_send())
+                if dz != 0 or h != 0:
+                    when_there(dz, lambda: direct(dz, h, False).wait_send())
 
     rounds = max(gz_n - 2, 1).bit_length() - 1
     pl.semaphore_wait(barrier, count)
-    if rounds > 0:
-        pass_token(0)
     gather()
-
-    for q in range(WINDOW):
-        for k, (yp, xp) in enumerate(YX):
-            for g in range(gy_n):
-                f[q % 2][yp, xp, q // 2, g * y2 : (g + 1) * y2, :] = got[g, q, k * y2 : (k + 1) * y2, :]
 
     run0(v, f, z0, z_count, 0, 0, EVENS, PHASE_A, 0)
     run0(v, f, z0, z_count, 1, 0, ODDS, PHASE_B, 1)
@@ -340,21 +360,31 @@
         def _(low=low, n=n):
             f1[low : low + n] = jnp.zeros((n,) + f1.shape[1:], F32)
 
-    def near(slot, dz):
+    sender = lax.rem(gy, 2) == 1
+    slots2 = {dz: slot for slot, dz in enumerate((-1, 1, -2, 2))}
+
+    def near(dz, target, mate):
         first, n, to = moves2[dz]
         return pltpu.make_async_remote_copy(
             src_ref=f1.at[pl.ds(3 + first, n)], dst_ref=f1.at[pl.ds(to, n)],
-            send_sem=ssem.at[slot], recv_sem=r2.at[slot],
-            device_id=(gz + dz, gy), device_id_type=MESH,
+            send_sem=ssem.at[2 * slots2[dz] + mate], recv_sem=r2.at[slots2[dz]],
+            device_id=(gz + dz, target), device_id_type=MESH,
         )
 
-    far_first = sorted(moves2, key=lambda d: -abs(d))
-    for slot, dz in enumerate(far_first):
-        when_there(dz, lambda: near(slot, dz).start())
-    for slot, dz in enumerate(far_first):
-        when_there(-dz, lambda: near(slot, dz).wait_recv())
-    for slot, dz in enumerate(far_first):
-        when_there(dz, lambda: near(slot, dz).wait_send())
+    def send_near(parity):
+        far = -1 if parity == 0 else 1
+        for dz in (far, 2 * far, -2 * far, -far):
+            when_there(dz, lambda: [near(dz, g, mate).start() for mate, g in ((1, gy), (0, sibling))])
+
+    if rounds > 0:
+        take_token(0)
+    if rounds > 1:
+        pass_token(1)
+    when(sender, lambda: each_parity(gz, send_near))
+    for dz in moves2:
+        when_there(-dz, lambda: near(dz, gy, 0).wait_recv())
+    for dz in moves2:
+        when(sender & there(dz), lambda: [near(dz, gy, mate).wait_send() for mate in (0, 1)])
 
     for r in range(1, rounds):
         take_token(r)
@@ -419,19 +449,18 @@
             acc = add(acc, total[0, r : r + 8, :])
         part[pl.ds(j, 1), :] = jnp.sum(acc, axis=0, keepdims=True)
 
-    sends, receives = [], []
-    for d in range(1, gz_n):
-        to = lax.rem(gz + d, gz_n)
-        sends.append(pltpu.make_async_remote_copy(
-            src_ref=part, dst_ref=parts.at[gz], send_sem=ssem.at[d - 1], recv_sem=r3.at[gz],
-            device_id=(to, gy), device_id_type=MESH,
-        ))
-        receives.append(pltpu.make_async_remote_copy(
-            src_ref=part, dst_ref=parts.at[to], send_sem=ssem.at[d - 1], recv_sem=r3.at[to],
-            device_id=(to, gy), device_id_type=MESH,
-        ))
-    for c in sends:
-        c.start()
+    def spread(d, target):
+        return pltpu.make_async_remote_copy(
+            src_ref=part, dst_ref=parts.at[gz], send_sem=rs, recv_sem=r3,
+            device_id=(lax.rem(gz + d, gz_n), target), device_id_type=MESH,
+        )
+
+    @pl.when(sender)
+    def _():
+        for d in sorted(range(1, gz_n), key=lambda d: -min(d, gz_n - d) if gz_n > 8 else -d):
+            for g in (sibling, gy):
+                spread(d, g).start()
+
     parts[gz] = part[...]
 
     back = permutation(nx, True)
@@ -447,17 +476,14 @@
             jnp.concatenate([flat[0], flat[1]], axis=1), back, precision=lax.Precision.HIGHEST, preferred_element_type=F32
         ).reshape(zl, yl, nx)
 
-    for c in receives:
-        c.wait_recv()
-    for c in sends:
-        c.wait_send()
+    others = parts.at[pl.ds(0, gz_n - 1)]
+    pltpu.make_async_copy(others, others, r3).wait()
+    when(sender, lambda: [pltpu.make_async_copy(others, others, rs).wait() for _ in range(2)])
     sums = parts[0]
     for d in range(1, gz_n):
         sums = sums + parts[d]
     alpha = jnp.sum(sums[0:1], axis=1, keepdims=True) / jnp.sum(sums[1:2], axis=1, keepdims=True)
-    alpha = alpha.reshape(1, 1, 1)
-    sol_ref[...] = sol_ref[...] * alpha
-    res_ref[...] = rhs_ref[...] - res_ref[...] * alpha
+    alpha_ref[...] = jnp.broadcast_to(alpha.reshape(1, 1), alpha_ref.shape)
 
 
 def solution(mesh):
@@ -470,11 +496,11 @@
         zc, yc = zl // 2, y2 // 2
         vmem = lambda *shape: pltpu.VMEM(shape, F32)
         dma = lambda *shape: pltpu.SemaphoreType.DMA(shape)
-        return pl.pallas_call(
+        p, image, alpha = pl.pallas_call(
             functools.partial(kernel, gz_n, gy_n),
-            out_shape=[vmem(*rhs.shape)] * 2,
+            out_shape=[vmem(*rhs.shape)] * 2 + [vmem(yl, nx)],
             in_specs=[pl.BlockSpec(memory_space=pl.ANY)],
-            out_specs=[pl.BlockSpec(memory_space=pltpu.VMEM)] * 2,
+            out_specs=[pl.BlockSpec(memory_space=pltpu.VMEM)] * 3,
             scratch_shapes=[
                 vmem(2, zl * yl, x2),
                 vmem(zl, 4 * y2, x2),
@@ -491,12 +517,13 @@
                 vmem(2, x2),
                 vmem(gz_n, 2, x2),
                 vmem(2, 2, zl, y_half, x2),
-                dma(max(6 * (gy_n // 2), gz_n)), dma(3, gy_n), dma(4), dma(gz_n),
+                dma(max(6 * (gy_n // 2), 8)), dma(3, gy_n), dma(4), pltpu.SemaphoreType.DMA, pltpu.SemaphoreType.DMA,
                 vmem(zl, yl, nx), pltpu.SemaphoreType.DMA,
                 pltpu.SemaphoreType.REGULAR((max(1, max(gz_n - 2, 1).bit_length() - 1),)),
             ],
             compiler_params=pltpu.CompilerParams(has_side_effects=True, collective_id=0),
         )(rhs)
+        return p * alpha, rhs - image * alpha
 
     return jax.shard_map(
         lambda rhs: tuple(body(rhs)),

time: 25.4 us -> 23.4 us (0.921)
  Pallas kernels: 23.4 us -> 21.9 us
  local copies, waits for them, and re-layouts: 1.26 us -> 0.01 us
  other arithmetic: 0 us -> 0.67 us
    pallas_call x1, Pallas kernels: 23.4 us -> 21.9 us  [body(): pl.pallas_call(functools.partial(kernel, gz_n, gy_n), out_shape=[vmem(*rh...]
    unnamed x2, local copies, waits for them, and re-layouts: 1.26 us -> 0.01 us
    sub x0 -> x1, other arithmetic: none -> 0.67 us  [body(): return (p * alpha, rhs - image * alpha)]
where the time goes in v2:
time: 23.4 us; the launch traced here: 23.2 us
  Pallas kernels  21.9 us (94%)
  other arithmetic  0.67 us (3%)
  between operations  0.65 us (3%)
    pallas_call x1, Pallas kernels, body(): pl.pallas_call(functools.partial(kernel, gz_n, gy_n), out_shape=[vmem(*rh...  21.9 us
    sub x1, other arithmetic, body(): return (p * alpha, rhs - image * alpha)  0.67 us

profile of v2, /device:TPU:0, one launch (start us, length us, event | category | flops | bytes accessed | tf_op | source)
XLA Modules:
  0.0 23.2 jit_solution(8324701883576218707)
XLA Ops:
  0.6 0.0 copy-start
  0.6 21.9 %shard_map.30 = (f32[8,8,256]{2,1,0:T(8,128)S(1)}, f32[8,8,256]{2,1,0:T(8,128)S(1)}, f32[8,256]{1,0:T(8,128)S(1)}) custom-call(f32[8,8,256]{2,1,0:T(8,128)} %rhs_hbm.1), custom_call_target="tpu_custom_call" | custom-call | tf_op jit(solution)/shard_map/pallas_call | solution.py:499
  22.6 0.0 copy-done
  22.6 0.7 %multiply_subtract_fusion = (f32[8,8,256]{2,1,0:T(8,128)}, f32[8,8,256]{2,1,0:T(8,128)}) fusion(f32[8,8,256]{2,1,0:T(8,128)S(1)} %copy-done, f32[8,8,256]{2,1,0:T(8,128)S(1)} %get-tuple-element.7, f32[8,256]{1,0:T(8,128)S(1)} %get-tuple-element.6, f32[8,8,256]{2,1,0:T(8,128)S(1)} %get-tuple-element.5), kind=kLoop, calls=%fused_computation | loop fusion | flops 49152 | bytes 335872 | tf_op jit(solution)/shard_map/sub | solution.py:526
Async XLA Ops:
  0.6 21.9 %copy-start = (f32[8,8,256]{2,1,0:T(8,128)S(1)}, f32[8,8,256]{2,1,0:T(8,128)}, u32[]{:S(2)}) copy-start(f32[8,8,256]{2,1,0:T(8,128)} %rhs_hbm.1) | copy-start | bytes 196612

commit v3 on v2

--- a/solution.py
+++ b/solution.py
@@ -58,11 +58,14 @@
     return [[add(tall[yp][xp], pair_sum(tall[yp][1 - xp], xp, 2)) for xp in (0, 1)] for yp in (0, 1)]
 
 
-def edge_twice(x, axis, width, at_end):
+def edge_some(x, axis, width, inner, outer, at_start, at_end):
     size = x.shape[axis]
     index = lax.broadcasted_iota(jnp.int32, x.shape, axis)
-    inner = index < size - width if at_end else index >= width
-    return x * jnp.where(inner, F32(2.0), F32(1.0))
+    edge = (index < width) if at_start else None
+    if at_end:
+        last = index >= size - width
+        edge = last if edge is None else edge | last
+    return x * jnp.where(edge, F32(outer), F32(inner))
 
 
 def phase0(v, f, zs, scale, steps):
@@ -76,10 +79,14 @@
         q = add(w[a], h * scale)
         u_near = shift(u, 2, near)
         v[yp][a] = add(h, u, u_near) * scale
-        twice = None if u is None else add(edge_twice(u, 2, 1, a == 0), u_near, shift(u, 2, far)) * scale
-        v[yp][b] = add(f[yp][b], w[b], q, shift(q, 2, far), twice) * scale
+        twice = None if u is None else add(edge_some(u, 2, 1, 2.0, 1.0, a == 1, a == 0), u_near, shift(u, 2, far)) * scale
+        q_far = shift(q, 2, far)
         if len(order) == 3:
-            v[yp][a] = add(h, pair_sum(add(w[b], v[yp][b]), a, 2)) * scale
+            p = add(w[b], add(f[yp][b], w[b]) * scale)
+            back = add(edge_some(q, 2, 1, 2.0, 1.0, a == 0, a == 1), q_far, shift(q, 2, near))
+            thrice = add(edge_some(u, 2, 1, 3.0, 2.0, True, True), F32(3.0) * u_near, shift(u, 2, far), shift(u, 2, 2 * near))
+            v[yp][a] = add(h, p, shift(p, 2, near), add(back, thrice * scale) * scale) * scale
+        v[yp][b] = add(f[yp][b], w[b], q, q_far, twice) * scale
     return v
 
 
@@ -93,12 +100,21 @@
     first = parity == a
     h = add(g, w)
     u = add(w, v)
-    m = jnp.where(first, add(w, h * scale), 0.0 if u is None else u)
-    second = add(edge_twice(m, 2, step, b == 1), both_sides(m, 2, 2 * step)) * jnp.where(first, F32(0.0), scale)
-    new = add(h, both_sides(m, 2, step), second) * scale
-    if len(order) == 3:
-        new = jnp.where(first, add(h, both_sides(add(w, new), 2, step)) * scale, new)
-    return new
+    q = add(w, h * scale)
+    if len(order) == 2:
+        m = jnp.where(first, q, 0.0 if u is None else u)
+        second = add(edge_some(m, 2, step, 2.0, 1.0, b == 0, b == 1), both_sides(m, 2, 2 * step))
+        return add(h, both_sides(m, 2, step), second * jnp.where(first, F32(0.0), scale)) * scale
+    m = jnp.where(first, q, u)
+    second = add(edge_some(m, 2, step, 2.0, 1.0, True, True), both_sides(m, 2, 2 * step))
+    here, there = (-step, step) if a == 0 else (step, -step)
+    index = lax.broadcasted_iota(jnp.int32, scale.shape, 2)
+    ends = (index < 2 * step) | (index >= scale.shape[2] - 2 * step)
+    thrice = add(
+        shift(u, 2, here) * jnp.where(ends, F32(2.0), F32(3.0)), F32(3.0) * shift(u, 2, there), both_sides(u, 2, 3 * step)
+    )
+    third = second + jnp.where(first, scale, F32(0.0)) * thrice
+    return add(h, both_sides(q, 2, step), third * scale) * scale
 
 
 def phase1(v, g, zs, scale, steps):
@@ -152,7 +168,7 @@
     for at, n in chunks(low, high, CHUNK1):
         here = pl.ds(at, n)
         below, above = (pl.ds(at, n), pl.ds(at + 1, n)) if odd else (pl.ds(at - 1, n), pl.ds(at, n))
-        g = [f[here, odd, yp] for yp in (0, 1)]
+        g = [f[odd, here, yp] for yp in (0, 1)]
         scale = scale_rows(g[0].shape, z0 + 2 * at - LOW1 + odd, z_count)
         zs, old = NONE[0], NONE[0]
         if fresh > 0:
@@ -191,7 +207,7 @@
 def kernel(
     gz_n, gy_n, rhs_hbm, sol_ref, res_ref, alpha_ref,
     flat, mine, got, fe, fo, ve, vo, dbuf, f1, v1e, v1o, vc, part, parts, nat,
-    ssem, r1, r2, r3, rs, rhs_ref, s5, token,
+    ssem, r1, rr, s2, r2, r3, rs, rhs_ref, s5, token,
 ):
     gz, gy = lax.axis_index("gz"), lax.axis_index("gy")
     zl, yl, nx = rhs_ref.shape
@@ -241,20 +257,26 @@
     for z in range(zl):
         for yp, xp in YX:
             row = flat[xp, pl.ds(z * yl + yp, y2, stride=2), :]
-            mine[z, (yp * 2 + xp) * y2 : (yp * 2 + xp + 1) * y2, :] = row
-    got[gy, pl.ds(LOW0, zl)] = mine[...]
-
-    @pl.when(gz == 0)
-    def _():
-        got[:, 0:LOW0] = jnp.zeros((gy_n, LOW0) + got.shape[2:], F32)
-
-    @pl.when(gz == gz_n - 1)
-    def _():
-        got[:, LOW0 + zl :] = jnp.zeros((gy_n, WINDOW - LOW0 - zl) + got.shape[2:], F32)
-
-    high = WINDOW - LOW0 - zl
-    moves1 = {-1: (0, high, LOW0 + zl), 0: (0, zl, LOW0), 1: (zl - LOW0, LOW0, 0)}
+            mine[z % 2, z // 2, (yp * 2 + xp) * y2 : (yp * 2 + xp + 1) * y2, :] = row
+
+    low = LOW0 // 2
+    counts = (EVENS, ODDS)
+    moves1 = [
+        {1: (zc - low, low, 0), 0: (0, zc, low), -1: (0, counts[zp] - low - zc, low + zc)} for zp in (0, 1)
+    ]
     moves2 = {-2: (0, zc // 2, 7), -1: (0, zc // 2, 5), 1: (0, zc // 2, 1), 2: (zc // 2 - 1, 1, 0)}
+
+    def rows(zp, dz):
+        _, n, to = moves1[zp][dz]
+        return pl.ds(to + zp * EVENS, n)
+
+    for zp in (0, 1):
+        got[gy, rows(zp, 0)] = mine[zp]
+        for dz, edge in ((1, 0), (-1, gz_n - 1)):
+
+            @pl.when(gz == edge)
+            def _(zp=zp, dz=dz):
+                got[:, rows(zp, dz)] = jnp.zeros((gy_n, moves1[zp][dz][1]) + got.shape[2:], F32)
 
     def pass_token(round_):
         reach = 2 << round_
@@ -271,77 +293,94 @@
         for parity in (0, 1):
             when(lax.rem(index, 2) == parity, lambda parity=parity: act(parity))
 
-    def unpack(dz, g):
-        _, n, to = moves1[dz]
-        for q in range(to, to + n):
+    def edges(act):
+        when(gz == 0, lambda: act(0))
+        when(gz == gz_n - 1, lambda: act(1))
+        when((gz > 0) & (gz < gz_n - 1), lambda: act(None))
+
+    def unpack(zp, dz, g):
+        _, n, to = moves1[zp][dz]
+        for i in range(to, to + n):
             for k, (yp, xp) in enumerate(YX):
-                f[q % 2][yp, xp, q // 2, g * y2 : (g + 1) * y2, :] = got[g, q, k * y2 : (k + 1) * y2, :]
+                f[zp][yp, xp, i, g * y2 : (g + 1) * y2, :] = got[g, i + zp * EVENS, k * y2 : (k + 1) * y2, :]
+
+    slots = {1: 0, -1: 1, 0: 2}
+
+    def direct(zp, dz, h, owner):
+        first, n, _ = moves1[zp][dz]
+        g = lax.rem(gy + 2 * h, gy_n)
+        source = g if owner else gy
+        return pltpu.make_async_remote_copy(
+            src_ref=mine.at[zp, pl.ds(first, n)],
+            dst_ref=got.at[source, rows(zp, dz)],
+            send_sem=ssem.at[0],
+            recv_sem=r1.at[zp, slots[dz], lax.div(source, 2)],
+            device_id=(gz - dz if owner else gz + dz, g),
+            device_id_type=MESH,
+        )
+
+    def relay(zp, dz, h):
+        place = got.at[lax.rem(gy + 2 * h, gy_n), rows(zp, dz)]
+        return pltpu.make_async_remote_copy(
+            src_ref=mine.at[zp] if dz == 0 and h == 0 else place,
+            dst_ref=place,
+            send_sem=ssem.at[1],
+            recv_sem=rr.at[zp],
+            device_id=(gz, sibling),
+            device_id_type=MESH,
+        )
+
+    def wait_rows(sem, n):
+        block = got.at[pl.ds(0, halves), pl.ds(0, n)]
+        pltpu.make_async_copy(block, block, sem).wait()
 
     def gather():
-        slots = {1: 0, -1: 1, 0: 2}
-
-        def direct(dz, h, owner):
-            first, n, to = moves1[dz]
-            g = lax.rem(gy + 2 * h, gy_n)
-            return pltpu.make_async_remote_copy(
-                src_ref=mine.at[pl.ds(first, n)],
-                dst_ref=got.at[g if owner else gy, pl.ds(to, n)],
-                send_sem=ssem.at[slots[dz] * halves + h],
-                recv_sem=r1.at[slots[dz], g if owner else gy],
-                device_id=(gz - dz if owner else gz + dz, g),
-                device_id_type=MESH,
-            )
-
-        def relay(dz, h, owner):
-            _, n, to = moves1[dz]
-            g = lax.rem((sibling if owner else gy) + 2 * h, gy_n)
-            place = got.at[g, pl.ds(to, n)]
-            return pltpu.make_async_remote_copy(
-                src_ref=mine if dz == 0 and h == 0 else place,
-                dst_ref=place,
-                send_sem=ssem.at[(3 + slots[dz]) * halves + h],
-                recv_sem=r1.at[slots[dz], g],
-                device_id=(gz, sibling),
-                device_id_type=MESH,
-            )
-
         def sends(parity):
             far = -1 if parity == 0 else 1
-            for dz, h in send_order(far, halves):
-                when_there(dz, lambda: direct(dz, h, False).start())
+            for zp in (0, 1):
+                for dz, h in send_order(far, halves):
+                    when_there(dz, lambda: direct(zp, dz, h, False).start())
+                relay(zp, 0, 0).start()
 
         each_parity(gz, sends)
-        relay(0, 0, False).start()
 
         def forwards(parity):
             far = 1 if parity == 0 else -1
-            for dz, h in receive_order(far, halves):
-
-                def go():
-                    direct(dz, h, True).wait_recv()
-                    relay(dz, h, False).start()
-
-                when_there(-dz, go)
+            for zp in (0, 1):
+                for dz, h in receive_order(far, halves):
+
+                    def go():
+                        direct(zp, dz, h, True).wait_recv()
+                        relay(zp, dz, h).start()
+
+                    when_there(-dz, go)
 
         each_parity(gz, forwards)
         if rounds > 0:
             pass_token(0)
-        each_parity(gy, lambda parity: [unpack(dz, g) for dz in (0, 1, -1) for g in range(parity, gy_n, 2)])
-        for dz in (0, 1, -1):
-            for h in range(halves):
-                when_there(-dz, lambda: relay(dz, h, True).wait_recv())
-            each_parity(gy, lambda parity: [unpack(dz, g) for g in range(1 - parity, gy_n, 2)])
-        for dz in (0, 1, -1):
-            for h in range(halves):
-                when_there(-dz, lambda: relay(dz, h, False).wait_send())
-                if dz != 0 or h != 0:
-                    when_there(dz, lambda: direct(dz, h, False).wait_send())
+        each_parity(gy, lambda parity: [
+            unpack(zp, dz, g) for zp in (0, 1) for dz in (0, 1, -1) for g in range(parity, gy_n, 2)
+        ])
+
+    def relayed(zp):
+        total = counts[zp]
+        less = (moves1[zp][1][1], moves1[zp][-1][1])
+        edges(lambda edge: wait_rows(rr.at[zp], total - (0 if edge is None else less[edge])))
+        each_parity(gy, lambda parity: [unpack(zp, dz, g) for dz in (0, 1, -1) for g in range(1 - parity, gy_n, 2)])
+
+    def sent():
+        up, down = (sum(moves1[zp][dz][1] for zp in (0, 1)) for dz in (1, -1))
+        own_rows = zl - zl // halves
+        edges(lambda edge: wait_rows(ssem.at[0], own_rows + (down if edge != 0 else 0) + (up if edge != 1 else 0)))
+        edges(lambda edge: wait_rows(ssem.at[1], zl + (up if edge != 0 else 0) + (down if edge != 1 else 0)))
 
     rounds = max(gz_n - 2, 1).bit_length() - 1
     pl.semaphore_wait(barrier, count)
     gather()
 
+    relayed(0)
     run0(v, f, z0, z_count, 0, 0, EVENS, PHASE_A, 0)
+    relayed(1)
     run0(v, f, z0, z_count, 1, 0, ODDS, PHASE_B, 1)
     run0(v, f, z0, z_count, 0, 1, EVENS - 1, PHASE_C, 2)
 
@@ -353,46 +392,52 @@
     half = gy_n * yc
     for z in range(zc):
         for yp in (0, 1):
-            f1[3 + z // 2, z % 2, yp] = dbuf[z, pl.ds(yp, half, stride=2), :]
+            f1[z % 2, 3 + z // 2, yp] = dbuf[z, pl.ds(yp, half, stride=2), :]
     for edge, low, n in ((0, 0, 3), (1, 0, 1), (gz_n - 2, 7, 2), (gz_n - 1, 5, 4)):
 
         @pl.when(gz == edge)
         def _(low=low, n=n):
-            f1[low : low + n] = jnp.zeros((n,) + f1.shape[1:], F32)
+            f1[:, low : low + n] = jnp.zeros((2, n) + f1.shape[2:], F32)
 
     sender = lax.rem(gy, 2) == 1
-    slots2 = {dz: slot for slot, dz in enumerate((-1, 1, -2, 2))}
-
-    def near(dz, target, mate):
+    def near(zp, dz, target):
         first, n, to = moves2[dz]
+        n = min(n, counts[zp] - to)
         return pltpu.make_async_remote_copy(
-            src_ref=f1.at[pl.ds(3 + first, n)], dst_ref=f1.at[pl.ds(to, n)],
-            send_sem=ssem.at[2 * slots2[dz] + mate], recv_sem=r2.at[slots2[dz]],
+            src_ref=f1.at[zp, pl.ds(3 + first, n)], dst_ref=f1.at[zp, pl.ds(to, n)],
+            send_sem=s2.at[zp], recv_sem=r2.at[zp],
             device_id=(gz + dz, target), device_id_type=MESH,
         )
 
     def send_near(parity):
         far = -1 if parity == 0 else 1
-        for dz in (far, 2 * far, -2 * far, -far):
-            when_there(dz, lambda: [near(dz, g, mate).start() for mate, g in ((1, gy), (0, sibling))])
+        for zp in (0, 1):
+            for dz in (far, 2 * far, -2 * far, -far):
+                when_there(dz, lambda: [near(zp, dz, g).start() for g in (gy, sibling)])
+
+    def wait_near(sem, sign, zps, times):
+        def take(missing):
+            n = sum(min(moves2[dz][1], counts[zp] - moves2[dz][2]) for zp in zps for dz in moves2 if dz not in missing)
+            block = f1.at[pl.ds(0, times), pl.ds(0, n)]
+            pltpu.make_async_copy(block, block, sem).wait()
+
+        low_side, high_side = (sign * 2, sign), (-sign * 2, -sign)
+        when(gz == 0, lambda: take(low_side))
+        when(gz == 1, lambda: take(low_side[:1]))
+        when(gz == gz_n - 2, lambda: take(high_side[:1]))
+        when(gz == gz_n - 1, lambda: take(high_side))
+        when((gz > 1) & (gz < gz_n - 2), lambda: take(()))
 
     if rounds > 0:
         take_token(0)
     if rounds > 1:
         pass_token(1)
     when(sender, lambda: each_parity(gz, send_near))
-    for dz in moves2:
-        when_there(-dz, lambda: near(dz, gy, 0).wait_recv())
-    for dz in moves2:
-        when(sender & there(dz), lambda: [near(dz, gy, mate).wait_send() for mate in (0, 1)])
-
-    for r in range(1, rounds):
-        take_token(r)
-        if r + 1 < rounds:
-            pass_token(r + 1)
-
+    sent()
     c0, c_count = gz * zc, gz_n * zc
+    wait_near(r2.at[0], 1, (0,), 1)
     run1(v1, f1, c0, c_count, 0, 0, EVENS, PHASE_A, 0)
+    wait_near(r2.at[1], 1, (1,), 1)
     run1(v1, f1, c0, c_count, 1, 0, ODDS, PHASE_B, 1)
     run1(v1, f1, c0, c_count, 0, 1, EVENS - 1, PHASE_C, 2)
 
@@ -400,7 +445,7 @@
     for i in range(1, EVENS - 1):
         s = [v1e[yp, pl.ds(i, 1)] + v1o[yp, pl.ds(i - 1, 1)] + v1o[yp, pl.ds(i, 1)] for yp in (0, 1)]
         tall = s[0] + pair_sum(s[1], 0, 1)
-        f2.append(f1[pl.ds(i, 1), 0, 0] - (27.0 * v1e[0, pl.ds(i, 1)] - (tall + both_sides(tall, 2, 1))))
+        f2.append(f1[0, pl.ds(i, 1), 0] - (27.0 * v1e[0, pl.ds(i, 1)] - (tall + both_sides(tall, 2, 1))))
     q0, q_count = gz * (zc // 2), gz_n * (zc // 2)
     f2e, f2o = f2[0::2], f2[1::2]
     scale2 = [scale_rows(f2[0].shape, q0 - LOW2 + i, q_count) for i in range(7)]
@@ -449,6 +494,11 @@
             acc = add(acc, total[0, r : r + 8, :])
         part[pl.ds(j, 1), :] = jnp.sum(acc, axis=0, keepdims=True)
 
+    for r in range(1, rounds):
+        take_token(r)
+        if r + 1 < rounds:
+            pass_token(r + 1)
+
     def spread(d, target):
         return pltpu.make_async_remote_copy(
             src_ref=part, dst_ref=parts.at[gz], send_sem=rs, recv_sem=r3,
@@ -478,6 +528,7 @@
 
     others = parts.at[pl.ds(0, gz_n - 1)]
     pltpu.make_async_copy(others, others, r3).wait()
+    when(sender, lambda: [wait_near(s2.at[zp], -1, (zp,), 2) for zp in (0, 1)])
     when(sender, lambda: [pltpu.make_async_copy(others, others, rs).wait() for _ in range(2)])
     sums = parts[0]
     for d in range(1, gz_n):
@@ -503,21 +554,22 @@
             out_specs=[pl.BlockSpec(memory_space=pltpu.VMEM)] * 3,
             scratch_shapes=[
                 vmem(2, zl * yl, x2),
-                vmem(zl, 4 * y2, x2),
+                vmem(2, zc, 4 * y2, x2),
                 vmem(gy_n, WINDOW, 4 * y2, x2),
                 vmem(2, 2, EVENS, y_half, x2),
                 vmem(2, 2, ODDS, y_half, x2),
                 vmem(2, 2, EVENS, y_half, x2),
                 vmem(2, 2, ODDS, y_half, x2),
                 vmem(zc, y_half, x2),
-                vmem(9, 2, 2, gy_n * yc, x2),
+                vmem(2, EVENS, 2, gy_n * yc, x2),
                 vmem(2, EVENS, gy_n * yc, x2),
                 vmem(2, ODDS, gy_n * yc, x2),
                 vmem(7, y_half, x2),
                 vmem(2, x2),
                 vmem(gz_n, 2, x2),
                 vmem(2, 2, zl, y_half, x2),
-                dma(max(6 * (gy_n // 2), 8)), dma(3, gy_n), dma(4), pltpu.SemaphoreType.DMA, pltpu.SemaphoreType.DMA,
+                dma(2), dma(2, 3, gy_n // 2), dma(2), dma(2), dma(2),
+                pltpu.SemaphoreType.DMA, pltpu.SemaphoreType.DMA,
                 vmem(zl, yl, nx), pltpu.SemaphoreType.DMA,
                 pltpu.SemaphoreType.REGULAR((max(1, max(gz_n - 2, 1).bit_length() - 1),)),
             ],

time: 23.4 us -> 22.7 us (0.970)
  Pallas kernels: 21.9 us -> 21.2 us
    pallas_call x1, Pallas kernels: 21.9 us -> 21.2 us  [body(): pl.pallas_call(functools.partial(kernel, gz_n, gy_n), out_shape=[vmem(*rh...]
where the time goes in v3:
time: 22.7 us; the launch traced here: 22.6 us
  Pallas kernels  21.2 us (93%)
  other arithmetic  0.67 us (3%)
  between operations  0.65 us (3%)
    pallas_call x1, Pallas kernels, body(): pl.pallas_call(functools.partial(kernel, gz_n, gy_n), out_shape=[vmem(*rh...  21.2 us
    sub x1, other arithmetic, body(): return (p * alpha, rhs - image * alpha)  0.67 us

profile of v3, /device:TPU:0, one launch (start us, length us, event | category | flops | bytes accessed | tf_op | source)
XLA Modules:
  0.0 22.6 jit_solution(13067971418877638057)
XLA Ops:
  0.6 0.0 copy-start
  0.6 21.2 %shard_map.30 = (f32[8,8,256]{2,1,0:T(8,128)S(1)}, f32[8,8,256]{2,1,0:T(8,128)S(1)}, f32[8,256]{1,0:T(8,128)S(1)}) custom-call(f32[8,8,256]{2,1,0:T(8,128)} %rhs_hbm.1), custom_call_target="tpu_custom_call" | custom-call | tf_op jit(solution)/shard_map/pallas_call | solution.py:550
  21.9 0.0 copy-done
  21.9 0.7 %multiply_subtract_fusion = (f32[8,8,256]{2,1,0:T(8,128)}, f32[8,8,256]{2,1,0:T(8,128)}) fusion(f32[8,8,256]{2,1,0:T(8,128)S(1)} %copy-done, f32[8,8,256]{2,1,0:T(8,128)S(1)} %get-tuple-element.7, f32[8,256]{1,0:T(8,128)S(1)} %get-tuple-element.6, f32[8,8,256]{2,1,0:T(8,128)S(1)} %get-tuple-element.5), kind=kLoop, calls=%fused_computation | loop fusion | flops 49152 | bytes 335872 | tf_op jit(solution)/shard_map/sub | solution.py:578
Async XLA Ops:
  0.6 21.2 %copy-start = (f32[8,8,256]{2,1,0:T(8,128)S(1)}, f32[8,8,256]{2,1,0:T(8,128)}, u32[]{:S(2)}) copy-start(f32[8,8,256]{2,1,0:T(8,128)} %rhs_hbm.1) | copy-start | bytes 196612

commit v4 on v3

--- a/solution.py
+++ b/solution.py
@@ -206,7 +206,7 @@
 
 def kernel(
     gz_n, gy_n, rhs_hbm, sol_ref, res_ref, alpha_ref,
-    flat, mine, got, fe, fo, ve, vo, dbuf, f1, v1e, v1o, vc, part, parts, nat,
+    flat, mine, plain, got, fe, fo, ve, vo, dbuf, f1, v1e, v1o, vc, part, parts, nat,
     ssem, r1, rr, s2, r2, r3, rs, rhs_ref, s5, token,
 ):
     gz, gy = lax.axis_index("gz"), lax.axis_index("gy")
@@ -258,25 +258,41 @@
         for yp, xp in YX:
             row = flat[xp, pl.ds(z * yl + yp, y2, stride=2), :]
             mine[z % 2, z // 2, (yp * 2 + xp) * y2 : (yp * 2 + xp + 1) * y2, :] = row
-
-    low = LOW0 // 2
+            plain[z, (yp * 2 + xp) * y2 : (yp * 2 + xp + 1) * y2, :] = row
+
+    parts1 = [
+        {1: (zc - 1, (-2,)), 0: (0, tuple(range(0, zl, 2))), -1: (0, (zl,))},
+        {1: (zc - 1, (-1,)), 0: (0, tuple(range(1, zl, 2)))},
+        {1: (zl - LOW0, tuple(range(-LOW0, -2))), -1: (1, tuple(range(zl + 1, WINDOW - LOW0)))},
+    ]
+    place_of, at = {}, 0
+    for part_ in parts1:
+        for dz, (_, zs) in part_.items():
+            for z in zs:
+                place_of[z] = at
+                at += 1
+    messages = [(k, dz, h) for k, part_ in enumerate(parts1) for dz in part_ for h in range(halves) if dz or h]
+    mail = {m: i for i, m in enumerate(messages)}
+    moves2 = {-2: (0, zc // 2, 7), -1: (0, zc // 2, 5), 1: (0, zc // 2, 1), 2: (zc // 2 - 1, 1, 0)}
     counts = (EVENS, ODDS)
-    moves1 = [
-        {1: (zc - low, low, 0), 0: (0, zc, low), -1: (0, counts[zp] - low - zc, low + zc)} for zp in (0, 1)
-    ]
-    moves2 = {-2: (0, zc // 2, 7), -1: (0, zc // 2, 5), 1: (0, zc // 2, 1), 2: (zc // 2 - 1, 1, 0)}
-
-    def rows(zp, dz):
-        _, n, to = moves1[zp][dz]
-        return pl.ds(to + zp * EVENS, n)
-
-    for zp in (0, 1):
-        got[gy, rows(zp, 0)] = mine[zp]
+
+    def rows(k, dz):
+        zs = parts1[k][dz][1]
+        return pl.ds(place_of[zs[0]], len(zs))
+
+    def outgoing(k, dz):
+        first, zs = parts1[k][dz]
+        return (plain if k == 2 else mine.at[k]).at[pl.ds(first, len(zs))]
+
+    for k in (0, 1):
+        got[gy, rows(k, 0)] = mine[k]
+    for k, part_ in enumerate(parts1):
         for dz, edge in ((1, 0), (-1, gz_n - 1)):
-
-            @pl.when(gz == edge)
-            def _(zp=zp, dz=dz):
-                got[:, rows(zp, dz)] = jnp.zeros((gy_n, moves1[zp][dz][1]) + got.shape[2:], F32)
+            if dz in part_:
+
+                @pl.when(gz == edge)
+                def _(k=k, dz=dz):
+                    got[:, rows(k, dz)] = jnp.zeros((gy_n, len(parts1[k][dz][1])) + got.shape[2:], F32)
 
     def pass_token(round_):
         reach = 2 << round_
@@ -298,34 +314,31 @@
         when(gz == gz_n - 1, lambda: act(1))
         when((gz > 0) & (gz < gz_n - 1), lambda: act(None))
 
-    def unpack(zp, dz, g):
-        _, n, to = moves1[zp][dz]
-        for i in range(to, to + n):
-            for k, (yp, xp) in enumerate(YX):
-                f[zp][yp, xp, i, g * y2 : (g + 1) * y2, :] = got[g, i + zp * EVENS, k * y2 : (k + 1) * y2, :]
-
-    slots = {1: 0, -1: 1, 0: 2}
-
-    def direct(zp, dz, h, owner):
-        first, n, _ = moves1[zp][dz]
+    def unpack(k, g):
+        for dz in parts1[k]:
+            for z in parts1[k][dz][1]:
+                for j, (yp, xp) in enumerate(YX):
+                    row = got[g, place_of[z], j * y2 : (j + 1) * y2, :]
+                    f[z % 2][yp, xp, (z + LOW0) // 2, g * y2 : (g + 1) * y2, :] = row
+
+    def direct(k, dz, h, owner):
         g = lax.rem(gy + 2 * h, gy_n)
-        source = g if owner else gy
         return pltpu.make_async_remote_copy(
-            src_ref=mine.at[zp, pl.ds(first, n)],
-            dst_ref=got.at[source, rows(zp, dz)],
+            src_ref=outgoing(k, dz),
+            dst_ref=got.at[g if owner else gy, rows(k, dz)],
             send_sem=ssem.at[0],
-            recv_sem=r1.at[zp, slots[dz], lax.div(source, 2)],
+            recv_sem=r1.at[mail[k, dz, (halves - h) % halves if owner else h]],
             device_id=(gz - dz if owner else gz + dz, g),
             device_id_type=MESH,
         )
 
-    def relay(zp, dz, h):
-        place = got.at[lax.rem(gy + 2 * h, gy_n), rows(zp, dz)]
+    def relay(k, dz, h):
+        place = got.at[lax.rem(gy + 2 * h, gy_n), rows(k, dz)]
         return pltpu.make_async_remote_copy(
-            src_ref=mine.at[zp] if dz == 0 and h == 0 else place,
+            src_ref=mine.at[k] if dz == 0 and h == 0 else place,
             dst_ref=place,
             send_sem=ssem.at[1],
-            recv_sem=rr.at[zp],
+            recv_sem=rr.at[k],
             device_id=(gz, sibling),
             device_id_type=MESH,
         )
@@ -334,57 +347,63 @@
         block = got.at[pl.ds(0, halves), pl.ds(0, n)]
         pltpu.make_async_copy(block, block, sem).wait()
 
-    def gather():
-        def sends(parity):
+    def send(ks):
+        def starts(parity):
             far = -1 if parity == 0 else 1
-            for zp in (0, 1):
+            for k in ks:
                 for dz, h in send_order(far, halves):
-                    when_there(dz, lambda: direct(zp, dz, h, False).start())
-                relay(zp, 0, 0).start()
-
-        each_parity(gz, sends)
-
+                    if dz in parts1[k]:
+                        when_there(dz, lambda: direct(k, dz, h, False).start())
+                if 0 in parts1[k]:
+                    relay(k, 0, 0).start()
+
+        each_parity(gz, starts)
+
+    def forward(ks):
         def forwards(parity):
             far = 1 if parity == 0 else -1
-            for zp in (0, 1):
+            for k in ks:
                 for dz, h in receive_order(far, halves):
 
                     def go():
-                        direct(zp, dz, h, True).wait_recv()
-                        relay(zp, dz, h).start()
-
-                    when_there(-dz, go)
+                        direct(k, dz, h, True).wait_recv()
+                        relay(k, dz, h).start()
+
+                    if dz in parts1[k]:
+                        when_there(-dz, go)
 
         each_parity(gz, forwards)
-        if rounds > 0:
-            pass_token(0)
-        each_parity(gy, lambda parity: [
-            unpack(zp, dz, g) for zp in (0, 1) for dz in (0, 1, -1) for g in range(parity, gy_n, 2)
-        ])
-
-    def relayed(zp):
-        total = counts[zp]
-        less = (moves1[zp][1][1], moves1[zp][-1][1])
-        edges(lambda edge: wait_rows(rr.at[zp], total - (0 if edge is None else less[edge])))
-        each_parity(gy, lambda parity: [unpack(zp, dz, g) for dz in (0, 1, -1) for g in range(1 - parity, gy_n, 2)])
+        each_parity(gy, lambda parity: [unpack(k, g) for k in ks for g in range(parity, gy_n, 2)])
+
+    def height(k, dz):
+        return len(parts1[k][dz][1]) if dz in parts1[k] else 0
+
+    def relayed(k):
+        total = sum(height(k, dz) for dz in (-1, 0, 1))
+        less = (height(k, 1), height(k, -1))
+        edges(lambda edge: wait_rows(rr.at[k], total - (0 if edge is None else less[edge])))
+        each_parity(gy, lambda parity: [unpack(k, g) for g in range(1 - parity, gy_n, 2)])
 
     def sent():
-        up, down = (sum(moves1[zp][dz][1] for zp in (0, 1)) for dz in (1, -1))
+        up, down = (sum(height(k, dz) for k in range(3)) for dz in (1, -1))
         own_rows = zl - zl // halves
         edges(lambda edge: wait_rows(ssem.at[0], own_rows + (down if edge != 0 else 0) + (up if edge != 1 else 0)))
         edges(lambda edge: wait_rows(ssem.at[1], zl + (up if edge != 0 else 0) + (down if edge != 1 else 0)))
 
     rounds = max(gz_n - 2, 1).bit_length() - 1
     pl.semaphore_wait(barrier, count)
-    gather()
-
+    own = LOW0 // 2
+    last = own + zc
+    send((0, 1, 2))
+    forward((0, 1))
+    if rounds > 0:
+        pass_token(0)
     relayed(0)
-    run0(v, f, z0, z_count, 0, 0, EVENS, PHASE_A, 0)
+    run0(v, f, z0, z_count, 0, own - 1, last + 1, PHASE_A, 0)
     relayed(1)
-    run0(v, f, z0, z_count, 1, 0, ODDS, PHASE_B, 1)
-    run0(v, f, z0, z_count, 0, 1, EVENS - 1, PHASE_C, 2)
-
-    own = LOW0 // 2
+    run0(v, f, z0, z_count, 1, own - 1, last, PHASE_B, 1)
+    run0(v, f, z0, z_count, 0, own, last, PHASE_C, 2)
+
     here, below, above = pl.ds(own, zc), pl.ds(own - 1, zc), pl.ds(own, zc)
     s = [[ve[yp, xp, here] + vo[yp, xp, below] + vo[yp, xp, above] for xp in (0, 1)] for yp in (0, 1)]
     tall = [s[0][xp] + pair_sum(s[1][xp], 0, 1) for xp in (0, 1)]
@@ -433,6 +452,15 @@
     if rounds > 1:
         pass_token(1)
     when(sender, lambda: each_parity(gz, send_near))
+    forward((2,))
+    relayed(2)
+    for phase, odd, ranges in (
+        (PHASE_A, 0, ((0, own - 1), (last + 1, EVENS))),
+        (PHASE_B, 1, ((0, own - 1), (last, ODDS))),
+        (PHASE_C, 0, ((1, own), (last, EVENS - 1))),
+    ):
+        for low, high in ranges:
+            run0(v, f, z0, z_count, odd, low, high, phase, odd if phase is not PHASE_C else 2)
     sent()
     c0, c_count = gz * zc, gz_n * zc
     wait_near(r2.at[0], 1, (0,), 1)
@@ -499,17 +527,21 @@
         if r + 1 < rounds:
             pass_token(r + 1)
 
-    def spread(d, target):
+    def spread(to, target):
         return pltpu.make_async_remote_copy(
             src_ref=part, dst_ref=parts.at[gz], send_sem=rs, recv_sem=r3,
-            device_id=(lax.rem(gz + d, gz_n), target), device_id_type=MESH,
+            device_id=(to, target), device_id_type=MESH,
         )
 
     @pl.when(sender)
     def _():
-        for d in sorted(range(1, gz_n), key=lambda d: -min(d, gz_n - d) if gz_n > 8 else -d):
-            for g in (sibling, gy):
-                spread(d, g).start()
+        for to in range(gz_n):
+
+            def go():
+                for g in (sibling, gy):
+                    spread(to, g).start()
+
+            when(gz != to, go)
 
     parts[gz] = part[...]
 
@@ -555,6 +587,7 @@
             scratch_shapes=[
                 vmem(2, zl * yl, x2),
                 vmem(2, zc, 4 * y2, x2),
+                vmem(zl, 4 * y2, x2),
                 vmem(gy_n, WINDOW, 4 * y2, x2),
                 vmem(2, 2, EVENS, y_half, x2),
                 vmem(2, 2, ODDS, y_half, x2),
@@ -568,7 +601,7 @@
                 vmem(2, x2),
                 vmem(gz_n, 2, x2),
                 vmem(2, 2, zl, y_half, x2),
-                dma(2), dma(2, 3, gy_n // 2), dma(2), dma(2), dma(2),
+                dma(2), dma(7 * (gy_n // 2) - 2), dma(3), dma(2), dma(2),
                 pltpu.SemaphoreType.DMA, pltpu.SemaphoreType.DMA,
                 vmem(zl, yl, nx), pltpu.SemaphoreType.DMA,
                 pltpu.SemaphoreType.REGULAR((max(1, max(gz_n - 2, 1).bit_length() - 1),)),

time: 22.7 us -> 21.7 us (0.956)
  Pallas kernels: 21.2 us -> 20.2 us
    pallas_call x1, Pallas kernels: 21.2 us -> 20.2 us  [body(): pl.pallas_call(functools.partial(kernel, gz_n, gy_n), out_shape=[vmem(*rh...]
where the time goes in v4:
time: 21.7 us; the launch traced here: 21.5 us
  Pallas kernels  20.2 us (93%)
  other arithmetic  0.67 us (3%)
  between operations  0.65 us (3%)
    pallas_call x1, Pallas kernels, body(): pl.pallas_call(functools.partial(kernel, gz_n, gy_n), out_shape=[vmem(*rh...  20.2 us
    sub x1, other arithmetic, body(): return (p * alpha, rhs - image * alpha)  0.67 us

profile of v4, /device:TPU:0, one launch (start us, length us, event | category | flops | bytes accessed | tf_op | source)
XLA Modules:
  0.0 21.5 jit_solution(12141653020955269149)
XLA Ops:
  0.6 0.0 copy-start
  0.6 20.2 %shard_map.30 = (f32[8,8,256]{2,1,0:T(8,128)S(1)}, f32[8,8,256]{2,1,0:T(8,128)S(1)}, f32[8,256]{1,0:T(8,128)S(1)}) custom-call(f32[8,8,256]{2,1,0:T(8,128)} %rhs_hbm.1), custom_call_target="tpu_custom_call" | custom-call | tf_op jit(solution)/shard_map/pallas_call | solution.py:582
  20.9 0.0 copy-done
  20.9 0.7 %multiply_subtract_fusion = (f32[8,8,256]{2,1,0:T(8,128)}, f32[8,8,256]{2,1,0:T(8,128)}) fusion(f32[8,8,256]{2,1,0:T(8,128)S(1)} %copy-done, f32[8,8,256]{2,1,0:T(8,128)S(1)} %get-tuple-element.7, f32[8,256]{1,0:T(8,128)S(1)} %get-tuple-element.6, f32[8,8,256]{2,1,0:T(8,128)S(1)} %get-tuple-element.5), kind=kLoop, calls=%fused_computation | loop fusion | flops 49152 | bytes 335872 | tf_op jit(solution)/shard_map/sub | solution.py:611
Async XLA Ops:
  0.6 20.2 %copy-start = (f32[8,8,256]{2,1,0:T(8,128)S(1)}, f32[8,8,256]{2,1,0:T(8,128)}, u32[]{:S(2)}) copy-start(f32[8,8,256]{2,1,0:T(8,128)} %rhs_hbm.1) | copy-start | bytes 196612

commit v5 on v4

--- a/solution.py
+++ b/solution.py
@@ -77,16 +77,22 @@
         u = add(w[b], v[yp][b])
         h = add(f[yp][a], w[a])
         q = add(w[a], h * scale)
+        y_far = shift(q if u is None else q + u * scale, 2, far)
+        if u is None:
+            v[yp][a] = h * scale
+            v[yp][b] = add(f[yp][b], w[b], q, y_far) * scale
+            continue
         u_near = shift(u, 2, near)
-        v[yp][a] = add(h, u, u_near) * scale
-        twice = None if u is None else add(edge_some(u, 2, 1, 2.0, 1.0, a == 1, a == 0), u_near, shift(u, 2, far)) * scale
-        q_far = shift(q, 2, far)
         if len(order) == 3:
             p = add(w[b], add(f[yp][b], w[b]) * scale)
-            back = add(edge_some(q, 2, 1, 2.0, 1.0, a == 0, a == 1), q_far, shift(q, 2, near))
-            thrice = add(edge_some(u, 2, 1, 3.0, 2.0, True, True), F32(3.0) * u_near, shift(u, 2, far), shift(u, 2, 2 * near))
-            v[yp][a] = add(h, p, shift(p, 2, near), add(back, thrice * scale) * scale) * scale
-        v[yp][b] = add(f[yp][b], w[b], q, q_far, twice) * scale
+            x_near = shift(p + scale * (q + F32(3.0) * (scale * u)), 2, near)
+            thrice = edge_some(u, 2, 1, 3.0, 2.0, True, True) + shift(u, 2, 2 * near)
+            inner = edge_some(q, 2, 1, 2.0, 1.0, a == 0, a == 1) + y_far + scale * thrice
+            v[yp][a] = add(h, p, x_near, scale * inner) * scale
+        else:
+            v[yp][a] = add(h, u, u_near) * scale
+        twice = edge_some(u, 2, 1, 2.0, 1.0, a == 1, a == 0) + u_near
+        v[yp][b] = add(f[yp][b], w[b], q, y_far, twice * scale) * scale
     return v
 
 
@@ -101,20 +107,21 @@
     h = add(g, w)
     u = add(w, v)
     q = add(w, h * scale)
+    if u is None:
+        return add(h, both_sides(jnp.where(first, q, 0.0), 2, step)) * scale
+    m = jnp.where(first, q, u)
+    second = add(edge_some(m, 2, step, 2.0, 1.0, True, True), both_sides(m, 2, 2 * step)) * scale
     if len(order) == 2:
-        m = jnp.where(first, q, 0.0 if u is None else u)
-        second = add(edge_some(m, 2, step, 2.0, 1.0, b == 0, b == 1), both_sides(m, 2, 2 * step))
-        return add(h, both_sides(m, 2, step), second * jnp.where(first, F32(0.0), scale)) * scale
-    m = jnp.where(first, q, u)
-    second = add(edge_some(m, 2, step, 2.0, 1.0, True, True), both_sides(m, 2, 2 * step))
+        return add(h, both_sides(m, 2, step), jnp.where(first, 0.0, second)) * scale
     here, there = (-step, step) if a == 0 else (step, -step)
     index = lax.broadcasted_iota(jnp.int32, scale.shape, 2)
     ends = (index < 2 * step) | (index >= scale.shape[2] - 2 * step)
-    thrice = add(
-        shift(u, 2, here) * jnp.where(ends, F32(2.0), F32(3.0)), F32(3.0) * shift(u, 2, there), both_sides(u, 2, 3 * step)
-    )
-    third = second + jnp.where(first, scale, F32(0.0)) * thrice
-    return add(h, both_sides(q, 2, step), third * scale) * scale
+    square = scale * scale
+    some = square * u
+    m_here = jnp.where(first, q, q + some * jnp.where(ends, F32(2.0), F32(3.0)))
+    m_there = jnp.where(first, q, q + some * F32(3.0))
+    third = jnp.where(first, square * both_sides(u, 2, 3 * step), 0.0)
+    return add(h, shift(m_here, 2, here), shift(m_there, 2, there), second, third) * scale
 
 
 def phase1(v, g, zs, scale, steps):
@@ -195,7 +202,7 @@
 
 
 def send_order(far, halves):
-    order = [(dz, h) for dz in (far, 0, -far) for h in reversed(range(halves))]
+    order = [(dz, h) for dz in (0, far, -far) for h in reversed(range(halves))]
     return [(dz, h) for dz, h in order if dz != 0 or h != 0]
 
 
@@ -363,7 +370,9 @@
         def forwards(parity):
             far = 1 if parity == 0 else -1
             for k in ks:
-                for dz, h in receive_order(far, halves):
+                for i, (dz, h) in enumerate(receive_order(far, halves)):
+                    if k == 0 and ks[0] == 0 and i == 1:
+                        send((2,))
 
                     def go():
                         direct(k, dz, h, True).wait_recv()
@@ -394,7 +403,7 @@
     pl.semaphore_wait(barrier, count)
     own = LOW0 // 2
     last = own + zc
-    send((0, 1, 2))
+    send((0, 1))
     forward((0, 1))
     if rounds > 0:
         pass_token(0)

time: 21.7 us -> 21.5 us (level)
  no operation moved by 1% of the time
where the time goes in v5:
time: 21.5 us; the launch traced here: 21.4 us
  Pallas kernels  20 us (93%)
  other arithmetic  0.67 us (3%)
  between operations  0.65 us (3%)
    pallas_call x1, Pallas kernels, body(): pl.pallas_call(functools.partial(kernel, gz_n, gy_n), out_shape=[vmem(*rh...  20 us
    sub x1, other arithmetic, body(): return (p * alpha, rhs - image * alpha)  0.67 us

profile of v5, /device:TPU:0, one launch (start us, length us, event | category | flops | bytes accessed | tf_op | source)
XLA Modules:
  0.0 21.4 jit_solution(2115598751381939016)
XLA Ops:
  0.6 0.0 copy-start
  0.6 20.0 %shard_map.30 = (f32[8,8,256]{2,1,0:T(8,128)S(1)}, f32[8,8,256]{2,1,0:T(8,128)S(1)}, f32[8,256]{1,0:T(8,128)S(1)}) custom-call(f32[8,8,256]{2,1,0:T(8,128)} %rhs_hbm.1), custom_call_target="tpu_custom_call" | custom-call | tf_op jit(solution)/shard_map/pallas_call | solution.py:591
  20.7 0.0 copy-done
  20.7 0.7 %multiply_subtract_fusion = (f32[8,8,256]{2,1,0:T(8,128)}, f32[8,8,256]{2,1,0:T(8,128)}) fusion(f32[8,8,256]{2,1,0:T(8,128)S(1)} %copy-done, f32[8,8,256]{2,1,0:T(8,128)S(1)} %get-tuple-element.7, f32[8,256]{1,0:T(8,128)S(1)} %get-tuple-element.6, f32[8,8,256]{2,1,0:T(8,128)S(1)} %get-tuple-element.5), kind=kLoop, calls=%fused_computation | loop fusion | flops 49152 | bytes 335872 | tf_op jit(solution)/shard_map/sub | solution.py:620
Async XLA Ops:
  0.6 20.1 %copy-start = (f32[8,8,256]{2,1,0:T(8,128)S(1)}, f32[8,8,256]{2,1,0:T(8,128)}, u32[]{:S(2)}) copy-start(f32[8,8,256]{2,1,0:T(8,128)} %rhs_hbm.1) | copy-start | bytes 196612

commit v6 on v5

--- a/solution.py
+++ b/solution.py
@@ -242,11 +242,12 @@
     barrier = pltpu.get_barrier_semaphore()
     count = jnp.int32(0)
     greet = [(dz, 2 * h) for h in reversed(range(halves)) for dz in (-1, 1)] + [(-2, 0), (2, 0)] + [(0, dg) for dg in range(1, gy_n)]
-    for dz, dg in greet:
-
-        def go(dz=dz, dg=dg):
+    greet = [(dz, dg, gy) for dz, dg in greet] + [(dz, 2 * h, sibling) for h in range(1, halves) for dz in (-1, 1)]
+    for dz, dg, base in greet:
+
+        def go(dz=dz, dg=dg, base=base):
             pl.semaphore_signal(
-                barrier, inc=1, device_id=(gz + dz, lax.rem(gy + dg, gy_n)), device_id_type=MESH
+                barrier, inc=1, device_id=(gz + dz, lax.rem(base + dg, gy_n)), device_id_type=MESH
             )
 
         when_there(dz, go)

time: 21.5 us -> 21.3 us (level)
    pallas_call x1, Pallas kernels: 20 us -> 19.8 us  [body(): pl.pallas_call(functools.partial(kernel, gz_n, gy_n), out_shape=[vmem(*rh...]
where the time goes in v6:
time: 21.3 us; the launch traced here: 21.1 us
  Pallas kernels  19.8 us (93%)
  other arithmetic  0.67 us (3%)
  between operations  0.65 us (3%)
    pallas_call x1, Pallas kernels, body(): pl.pallas_call(functools.partial(kernel, gz_n, gy_n), out_shape=[vmem(*rh...  19.8 us
    sub x1, other arithmetic, body(): return (p * alpha, rhs - image * alpha)  0.67 us

profile of v6, /device:TPU:0, one launch (start us, length us, event | category | flops | bytes accessed | tf_op | source)
XLA Modules:
  0.0 21.1 jit_solution(13739558576417694077)
XLA Ops:
  0.6 0.0 copy-start
  0.6 19.8 %shard_map.30 = (f32[8,8,256]{2,1,0:T(8,128)S(1)}, f32[8,8,256]{2,1,0:T(8,128)S(1)}, f32[8,256]{1,0:T(8,128)S(1)}) custom-call(f32[8,8,256]{2,1,0:T(8,128)} %rhs_hbm.1), custom_call_target="tpu_custom_call" | custom-call | tf_op jit(solution)/shard_map/pallas_call | solution.py:592
  20.4 0.0 copy-done
  20.4 0.7 %multiply_subtract_fusion = (f32[8,8,256]{2,1,0:T(8,128)}, f32[8,8,256]{2,1,0:T(8,128)}) fusion(f32[8,8,256]{2,1,0:T(8,128)S(1)} %copy-done, f32[8,8,256]{2,1,0:T(8,128)S(1)} %get-tuple-element.7, f32[8,256]{1,0:T(8,128)S(1)} %get-tuple-element.6, f32[8,8,256]{2,1,0:T(8,128)S(1)} %get-tuple-element.5), kind=kLoop, calls=%fused_computation | loop fusion | flops 49152 | bytes 335872 | tf_op jit(solution)/shard_map/sub | solution.py:621
Async XLA Ops:
  0.6 19.8 %copy-start = (f32[8,8,256]{2,1,0:T(8,128)S(1)}, f32[8,8,256]{2,1,0:T(8,128)}, u32[]{:S(2)}) copy-start(f32[8,8,256]{2,1,0:T(8,128)} %rhs_hbm.1) | copy-start | bytes 196612

commit v7 on v6

--- a/solution.py
+++ b/solution.py
@@ -442,7 +442,7 @@
         far = -1 if parity == 0 else 1
         for zp in (0, 1):
             for dz in (far, 2 * far, -2 * far, -far):
-                when_there(dz, lambda: [near(zp, dz, g).start() for g in (gy, sibling)])
+                when_there(dz, lambda: near(zp, dz, gy).start())
 
     def wait_near(sem, sign, zps, times):
         def take(missing):
@@ -461,7 +461,7 @@
         take_token(0)
     if rounds > 1:
         pass_token(1)
-    when(sender, lambda: each_parity(gz, send_near))
+    each_parity(gz, send_near)
     forward((2,))
     relayed(2)
     for phase, odd, ranges in (
@@ -570,7 +570,7 @@
 
     others = parts.at[pl.ds(0, gz_n - 1)]
     pltpu.make_async_copy(others, others, r3).wait()
-    when(sender, lambda: [wait_near(s2.at[zp], -1, (zp,), 2) for zp in (0, 1)])
+    [wait_near(s2.at[zp], -1, (zp,), 1) for zp in (0, 1)]
     when(sender, lambda: [pltpu.make_async_copy(others, others, rs).wait() for _ in range(2)])
     sums = parts[0]
     for d in range(1, gz_n):

time: 21.3 us -> 21.2 us (level)
  no operation moved by 1% of the time
where the time goes in v7:
time: 21.2 us; the launch traced here: 21.1 us
  Pallas kernels  19.7 us (93%)
  other arithmetic  0.67 us (3%)
  between operations  0.65 us (3%)
    pallas_call x1, Pallas kernels, body(): pl.pallas_call(functools.partial(kernel, gz_n, gy_n), out_shape=[vmem(*rh...  19.7 us
    sub x1, other arithmetic, body(): return (p * alpha, rhs - image * alpha)  0.67 us

profile of v7, /device:TPU:0, one launch (start us, length us, event | category | flops | bytes accessed | tf_op | source)
XLA Modules:
  0.0 21.1 jit_solution(8422672225329862453)
XLA Ops:
  0.6 0.0 copy-start
  0.6 19.7 %shard_map.30 = (f32[8,8,256]{2,1,0:T(8,128)S(1)}, f32[8,8,256]{2,1,0:T(8,128)S(1)}, f32[8,256]{1,0:T(8,128)S(1)}) custom-call(f32[8,8,256]{2,1,0:T(8,128)} %rhs_hbm.1), custom_call_target="tpu_custom_call" | custom-call | tf_op jit(solution)/shard_map/pallas_call | solution.py:592
  20.4 0.0 copy-done
  20.4 0.7 %multiply_subtract_fusion = (f32[8,8,256]{2,1,0:T(8,128)}, f32[8,8,256]{2,1,0:T(8,128)}) fusion(f32[8,8,256]{2,1,0:T(8,128)S(1)} %copy-done, f32[8,8,256]{2,1,0:T(8,128)S(1)} %get-tuple-element.7, f32[8,256]{1,0:T(8,128)S(1)} %get-tuple-element.6, f32[8,8,256]{2,1,0:T(8,128)S(1)} %get-tuple-element.5), kind=kLoop, calls=%fused_computation | loop fusion | flops 49152 | bytes 335872 | tf_op jit(solution)/shard_map/sub | solution.py:621
Async XLA Ops:
  0.6 19.7 %copy-start = (f32[8,8,256]{2,1,0:T(8,128)S(1)}, f32[8,8,256]{2,1,0:T(8,128)}, u32[]{:S(2)}) copy-start(f32[8,8,256]{2,1,0:T(8,128)} %rhs_hbm.1) | copy-start | bytes 196612
